TPU v7x, 32 devices: a whole 2x2x4 slice. The times are simulated.
32 devices in a mesh: dp: 4 (over y, x), row: 2 (over core), col: 4 (over z).
Axes of the slice: x: 2, y: 2, z: 4, core: 2. Of those that a mesh axis runs over, the one named last changes fastest.
Arguments:
- x_in: bfloat16 [4096, 2048], P(('dp', 'col'), 'row'), may hold values from -6 to 6
- cotangent: bfloat16 [4096, 2048], P(('dp', 'col'), 'row'), may hold values from -6 to 6
- segment_ids: int32 [4, 1024], P('dp'), may hold values from 0 to 7, never falling along the last dimension, each value on 1 to 512 neighbouring positions
- owner: int32 [4], replicated, may hold values from 0 to 3, as said below
- w_mix_in: bfloat16 [2048, 8240], P('row', 'col'), may hold values from -0.125 to 0.125
- w_mix_out: bfloat16 [4096, 2048], P('col', 'row'), may hold values from -0.1875 to 0.1875
- w_gate_up: bfloat16 [2048, 8192], P('row', 'col'), may hold values from -0.125 to 0.125
- w_down: bfloat16 [4096, 2048], P('col', 'row'), may hold values from -0.09375 to 0.09375
- mat_m: float32 [2, 4, 4, 4218880], P('row', 'col', 'dp')
- mat_v: float32 [2, 4, 4, 4218880], P('row', 'col', 'dp'), as said below
- small_params: float32 [22160], replicated, as said below
- small_m: float32 [22160], replicated, may hold values from -128 to 128
- small_v: float32 [22160], replicated, may hold values from 100 to 10000
Outputs:
- y_out: bfloat16 [4096, 2048], P(('dp', 'col'), 'row')
- x_grad: bfloat16 [4096, 2048], P(('dp', 'col'), 'row')
- mat_grad: float32 [2, 4, 4, 4218880], P('row', 'col', 'dp')
- mat_m_new: float32 [2, 4, 4, 4218880], P('row', 'col', 'dp')
- mat_v_new: float32 [2, 4, 4, 4218880], P('row', 'col', 'dp')
- mat_update: float32 [2, 4, 4, 4218880], P('row', 'col', 'dp')
- new_mix_in: bfloat16 [2048, 8240], P('row', 'col')
- new_mix_out: bfloat16 [4096, 2048], P('col', 'row')
- new_gate_up: bfloat16 [2048, 8192], P('row', 'col')
- new_down: bfloat16 [4096, 2048], P('col', 'row')
- small_grad: float32 [22160], replicated
- small_m_new: float32 [22160], replicated
- small_v_new: float32 [22160], replicated
- small_update: float32 [22160], replicated
Inputs may be any that keep to these rules, and one draw needn't show every extreme that they name: owner[i] is an owner group; one group owns exactly 2 matrices, every other group at most one. `mat_v`: positive on the entries of owned blocks, zero elsewhere. `small_params`: gains near one, skip terms positive, convolution terms of any sign.
All inputs are finite; a program needn't handle non-finite values.
Results may differ from a plain program's by a relative error of at most 0.03.
Values may be sent and summed in bfloat16 or wider, within the bound.
A program may use at most 320 MiB of HBM per device.

v0:
```python
import jax
import jax.numpy as jnp
from jax import lax
from jax.sharding import PartitionSpec as P

D = 2048
FF = 4096
QH = 8
KVH = 2
HD = 128
SH = 48
SP = 64
STATE = 256
CONV = 4
SPAN = 128
SEQ = 1024
MATS = 4
OWNERS = 4
STEP = 4


highest = lax.Precision.HIGHEST
norm_eps = 1e-05
beta_one = 0.5
beta_two = 0.6
learn_rate = 0.02
adam_eps = 1e-08
weight_decay = 0.1
masked_score = -1e30


def entering(shard, axis, join, neutral):
    place = lax.axis_index(axis)
    gathered = jax.tree.map(
        lambda a, kind: lax.all_gather(a.astype(kind), axis), shard, (jnp.bfloat16, jnp.bfloat16)
    )
    state = jax.tree.map(lambda a, e: jnp.zeros_like(a) + jnp.asarray(e, a.dtype), shard, neutral)

    def one(hop, state):
        return join(
            state,
            jax.tree.map(
                lambda a, own: lax.dynamic_index_in_dim(a, hop, 0, False).astype(own.dtype),
                gathered,
                shard,
            ),
        )

    return lax.fori_loop(0, place, one, state)


def carried_in(shard, axis, combine, identity):
    size, here = (lax.axis_size(axis), lax.axis_index(axis))
    everything = jax.tree.map(
        lambda part, kind: lax.all_gather(part.astype(kind), axis),
        shard,
        jax.tree.map(lambda a: jnp.bfloat16 if a.dtype == jnp.float32 else a.dtype, shard),
    )
    start = jax.tree.map(
        lambda part, zero: jnp.broadcast_to(jnp.asarray(zero, part.dtype), part.shape),
        shard,
        identity,
    )

    def hop(k, before):
        at = size - 1 - k
        reached = at > here
        new = combine(
            before, jax.tree.map(lambda part, own: part[at].astype(own.dtype), everything, shard)
        )
        return jax.tree.map(lambda a, b: jnp.where(reached, a, b), new, before)

    return lax.fori_loop(0, size, hop, start)


def silu_value(values):
    return values * jax.nn.sigmoid(values)


def silu_slope(values):
    sigmoid = jax.nn.sigmoid(values)
    return sigmoid * (1.0 + values * (1.0 - sigmoid))


def adam_step(gradient, moment, second, weight):
    moment_new = beta_one * moment + (1.0 - beta_one) * gradient
    second_new = beta_two * second + (1.0 - beta_two) * gradient * gradient
    first_hat = moment_new / (1.0 - beta_one**STEP)
    second_hat = second_new / (1.0 - beta_two**STEP)
    update = -learn_rate * (first_hat / (jnp.sqrt(second_hat) + adam_eps) + weight_decay * weight)
    return (moment_new, second_new, update)


def gather_col(values):
    return lax.all_gather(values, "col", axis=0, tiled=True)


def sum_row(term_fn, row_total_count):
    return lax.psum_scatter(
        term_fn(jnp.int32(0), row_total_count * lax.axis_size("row")),
        "row",
        scatter_dimension=0,
        tiled=True,
    )


def gather_row(values):
    return lax.all_gather(values, "row", axis=0, tiled=True)


def sum_col(term_fn, row_total_count):
    return lax.psum_scatter(
        term_fn(jnp.int32(0), row_total_count * lax.axis_size("col")),
        "col",
        scatter_dimension=0,
        tiled=True,
    )


def row_total(values):
    return lax.psum(values, "row")


def rows_times(gathered, weight, transpose):

    def partial_rows(row_start, row_count):
        if transpose:
            return lax.dot_general(
                gathered, weight, (((1,), (1,)), ((), ())), preferred_element_type=jnp.float32
            )
        return jnp.dot(gathered, weight, preferred_element_type=jnp.float32)

    return partial_rows


def conv_rows(values, segments, kernel, out_rows):
    current = segments[CONV - 1 : CONV - 1 + out_rows]
    summed = values[CONV - 1 : CONV - 1 + out_rows] * kernel[0]
    for lag_steps in range(1, CONV):
        first = CONV - 1 - lag_steps
        keep_mask = (segments[first : first + out_rows] == current).astype(jnp.float32)
        summed = summed + kernel[lag_steps] * values[first : first + out_rows] * keep_mask[:, None]
    return summed


def conv_back(grads_padded, segments, kernel, out_rows):
    base_seg = segments[:out_rows]
    summed = grads_padded[:out_rows] * kernel[0]
    for lag_steps in range(1, CONV):
        keep_mask = (segments[lag_steps : lag_steps + out_rows] == base_seg).astype(jnp.float32)
        summed = (
            summed
            + kernel[lag_steps]
            * grads_padded[lag_steps : lag_steps + out_rows]
            * keep_mask[:, None]
        )
    return summed


def kernel_grad(grads_rows, pre_padded, seg_padded):
    row_count = grads_rows.shape[0]
    current = seg_padded[CONV - 1 : CONV - 1 + row_count]
    pieces = []
    for lag_steps in range(CONV):
        first = CONV - 1 - lag_steps
        keep_mask = (seg_padded[first : first + row_count] == current).astype(jnp.float32)
        pieces.append(
            jnp.sum(grads_rows * pre_padded[first : first + row_count] * keep_mask[:, None], 0)
        )
    return jnp.stack(pieces)


def scan_blocks(x_three, b_float, c_float, step_sizes, rate, segments, prev_seg, start_state):
    token_count = x_three.shape[0]
    block_count = token_count // SPAN

    def one_block(running_carry, inputs):
        state_now, last_seg = running_carry
        x_block, b_block, c_block, dt_block, seg_block = inputs
        log_decay = dt_block * rate
        running = jnp.cumsum(log_decay, axis=0)
        positions = jnp.arange(SPAN)
        live_pairs = (seg_block[:, None] == seg_block[None, :]) & (
            positions[:, None] >= positions[None, :]
        )
        decay_logs = running[:, None, :] - running[None, :, :]
        decay_table = jnp.where(
            live_pairs[:, :, None], jnp.exp(jnp.where(live_pairs[:, :, None], decay_logs, 0.0)), 0.0
        )
        intersection = jnp.dot(c_block, b_block.T, precision=highest)
        inflow = dt_block[:, :, None] * x_block
        output = jnp.einsum(
            "tsh,shp->thp", decay_table * intersection[:, :, None], inflow, precision=highest
        )
        carried = jnp.exp(running) * (seg_block == last_seg).astype(jnp.float32)[:, None]
        output = output + carried[:, :, None] * jnp.einsum(
            "hpn,tn->thp", state_now, c_block, precision=highest
        )
        tail_decay = (
            jnp.exp(running[-1][None, :] - running)
            * (seg_block == seg_block[-1]).astype(jnp.float32)[:, None]
        )
        fresh_state = jnp.einsum("sh,shp,sn->hpn", tail_decay, inflow, b_block, precision=highest)
        passing = jnp.exp(running[-1]) * (seg_block[-1] == last_seg).astype(jnp.float32)
        return ((passing[:, None, None] * state_now + fresh_state, seg_block[-1]), output)

    inputs = (
        x_three.reshape(block_count, SPAN, x_three.shape[1], x_three.shape[2]),
        b_float.reshape(block_count, SPAN, b_float.shape[1]),
        c_float.reshape(block_count, SPAN, c_float.shape[1]),
        step_sizes.reshape(block_count, SPAN, step_sizes.shape[1]),
        segments.reshape(block_count, SPAN),
    )
    (state_end, last_seg), outputs = lax.scan(one_block, (start_state, prev_seg), inputs)
    return (outputs.reshape(x_three.shape), state_end)


def chain_states(earlier, later):
    return (earlier[0] * later[0], later[1] + later[0][:, None, None] * earlier[1])


def norm_back(grad_act, normed, scale_rows, gain):
    weighted = grad_act * gain
    inner_sum = row_total(jnp.sum(weighted * normed, 1))
    grad_in = scale_rows[:, None] * (weighted - normed * (inner_sum / D)[:, None])
    return (grad_in, jnp.sum(grad_act * normed, 0))


def shards(
    x_in,
    cotangent,
    segment_ids,
    owner,
    w_mix_in,
    w_mix_out,
    w_gate_up,
    w_down,
    mat_m,
    mat_v,
    small_params,
    small_m,
    small_v,
):
    n_row = lax.axis_size("row")
    n_col = lax.axis_size("col")
    n_dp = lax.axis_size("dp")
    row_index = lax.axis_index("row")
    col_index = lax.axis_index("col")
    dp_index = lax.axis_index("dp")
    tok_col, width_row = x_in.shape
    tok_row = SEQ // n_row
    q_width = QH * HD // n_col
    shared_width = 4 * STATE // n_col
    sub_width = STATE // n_col
    ssm_width = SH * SP // n_col
    head_count = SH // n_col
    ff_width = FF // n_col
    mix_width = q_width + ssm_width
    conv_width = SH * SP + 2 * STATE
    col_b = q_width + 2 * sub_width
    col_z = q_width + shared_width
    col_x = col_z + ssm_width
    col_dt = col_x + ssm_width
    segs = segment_ids[0]
    off_alog = 2 * D
    off_dtb = 2 * D + SH
    off_skip = 2 * D + 2 * SH
    off_kern = 2 * D + 3 * SH
    off_cbias = off_kern + CONV * conv_width
    gain_one = lax.dynamic_slice_in_dim(small_params, row_index * width_row, width_row)
    gain_two = lax.dynamic_slice_in_dim(small_params, D + row_index * width_row, width_row)
    a_log_own = lax.dynamic_slice_in_dim(
        small_params, off_alog + col_index * head_count, head_count
    )
    dt_bias_own = lax.dynamic_slice_in_dim(
        small_params, off_dtb + col_index * head_count, head_count
    )
    skip_own = lax.dynamic_slice_in_dim(small_params, off_skip + col_index * head_count, head_count)
    kernel_all = small_params[off_kern:off_cbias].reshape(CONV, conv_width)
    cbias_all = small_params[off_cbias : off_cbias + conv_width]

    def own_channels(table):
        last_axis = table.ndim - 1
        x_part = lax.dynamic_slice_in_dim(table, col_index * ssm_width, ssm_width, last_axis)
        b_part = lax.dynamic_slice_in_dim(
            table, SH * SP + col_index * sub_width, sub_width, last_axis
        )
        c_part = lax.dynamic_slice_in_dim(
            table, SH * SP + STATE + col_index * sub_width, sub_width, last_axis
        )
        return (x_part, b_part, c_part)

    kern_x, kern_b, kern_c = own_channels(kernel_all)
    bias_x, bias_b, bias_c = own_channels(cbias_all)
    kern_bc = jnp.concatenate([kern_b, kern_c], 1)
    seg_pad_top = jnp.concatenate([jnp.full((CONV - 1,), -1, jnp.int32), segs])
    seg_pad_bottom = jnp.concatenate([segs, jnp.full((CONV - 1,), -2, jnp.int32)])
    xf = x_in.astype(jnp.float32)
    scale_one = lax.rsqrt(row_total(jnp.sum(xf * xf, 1)) / D + norm_eps)
    normed_one = xf * scale_one[:, None]
    act_one = (normed_one * gain_one).astype(jnp.bfloat16)
    act_one_g = gather_col(act_one)
    act_one_pad = jnp.concatenate([jnp.zeros((CONV - 1, width_row), jnp.bfloat16), act_one_g], 0)

    def mix_in_term(row_start, row_count):
        raw_rows = jnp.dot(act_one_pad, w_mix_in, preferred_element_type=jnp.float32)
        plain_rows = raw_rows[CONV - 1 :]
        conv_bc = conv_rows(raw_rows[:, col_b:col_z], seg_pad_top, kern_bc, row_count)
        conv_x = conv_rows(raw_rows[:, col_x:col_dt], seg_pad_top, kern_x, row_count)
        return jnp.concatenate(
            [
                plain_rows[:, :col_b],
                conv_bc,
                plain_rows[:, col_z:col_x],
                conv_x,
                plain_rows[:, col_dt:],
            ],
            1,
        )

    projected = sum_row(mix_in_term, tok_row)
    own_start = row_index * tok_row
    own_segs = lax.dynamic_slice_in_dim(segs, own_start, tok_row)
    before_seg = lax.dynamic_slice_in_dim(segs, jnp.maximum(own_start - 1, 0), 1)[0]
    prev_seg = jnp.where(row_index > 0, before_seg, -1)
    queries = projected[:, :q_width].astype(jnp.bfloat16)
    keys_own = projected[:, q_width : q_width + sub_width]
    vals_own = projected[:, q_width + sub_width : col_b]
    b_pre = projected[:, col_b : col_b + sub_width] + bias_b
    c_pre = projected[:, col_b + sub_width : col_z] + bias_c
    z_gate = projected[:, col_z:col_x]
    x_pre = projected[:, col_x:col_dt] + bias_x
    dt_raw = projected[:, col_dt:]
    x_sig = silu_value(x_pre).astype(jnp.bfloat16)
    shared = jnp.concatenate([keys_own, vals_own, silu_value(b_pre), silu_value(c_pre)], 1).astype(
        jnp.bfloat16
    )
    features = lax.all_gather(shared, "col", axis=1, tiled=True)
    features = (
        features.reshape(tok_row, n_col, 4, sub_width)
        .transpose(0, 2, 1, 3)
        .reshape(tok_row, 4, STATE)
    )
    q_local = QH // n_col
    kv_head = col_index * q_local // (QH // KVH)
    key_head = lax.dynamic_slice_in_dim(features[:, 0], kv_head * HD, HD, 1)
    val_head = lax.dynamic_slice_in_dim(features[:, 1], kv_head * HD, HD, 1)
    b_float = features[:, 2].astype(jnp.float32)
    c_float = features[:, 3].astype(jnp.float32)
    key_all, val_all = (
        lax.all_gather(key_head, "row", axis=0, tiled=True),
        lax.all_gather(val_head, "row", axis=0, tiled=True),
    )
    q_heads = queries.reshape(tok_row, q_local, HD)
    score_scale = HD ** (-0.5)
    query_pos = own_start + jnp.arange(tok_row)
    key_pos = jnp.arange(SEQ)
    allowed = (key_pos[None, :] <= query_pos[:, None]) & (segs[None, :] == own_segs[:, None])

    def attn_scores():
        raw_scores = (
            jnp.einsum("qhd,kd->hqk", q_heads, key_all, preferred_element_type=jnp.float32)
            * score_scale
        )
        return jnp.where(allowed[None], raw_scores, masked_score)

    scores = attn_scores()
    top_score = jnp.max(scores, -1, keepdims=True)
    expo = jnp.exp(scores - top_score)
    expo_total = jnp.sum(expo, -1, keepdims=True)
    log_total = top_score + jnp.log(expo_total)
    probs_b = (expo / expo_total).astype(jnp.bfloat16)
    attended = jnp.einsum(
        "hqk,kd->qhd", probs_b, val_all, preferred_element_type=jnp.float32
    ).reshape(tok_row, q_width)
    x_three = x_sig.astype(jnp.float32).reshape(tok_row, head_count, SP)

    def scan_part(x_arg, b_arg, c_arg, dt_arg, bias_arg, alog_arg, skip_arg):
        step_sizes = jax.nn.softplus(dt_arg + bias_arg)
        rate = -jnp.exp(alog_arg)
        start_state = jnp.zeros((head_count, SP, STATE), jnp.float32)
        y_local, state_end = scan_blocks(
            x_arg, b_arg, c_arg, step_sizes, rate, own_segs, prev_seg, start_state
        )
        y_local = y_local + skip_arg[None, :, None] * x_arg
        passing = jnp.exp(jnp.sum(step_sizes * rate, 0)) * (own_segs[-1] == prev_seg).astype(
            jnp.float32
        )
        return (y_local, passing, state_end)

    def inflow_part(c_arg, dt_arg, bias_arg, alog_arg, state_arg):
        step_sizes = jax.nn.softplus(dt_arg + bias_arg)
        running = jnp.cumsum(step_sizes * -jnp.exp(alog_arg), axis=0)
        factor = jnp.exp(running) * (own_segs == prev_seg).astype(jnp.float32)[:, None]
        return factor[:, :, None] * jnp.einsum("hpn,tn->thp", state_arg, c_arg, precision=highest)

    (y_local, passing, state_end), scan_pull = jax.vjp(
        scan_part, x_three, b_float, c_float, dt_raw, dt_bias_own, a_log_own, skip_own
    )
    identity = (
        jnp.ones((head_count,), jnp.float32),
        jnp.zeros((head_count, SP, STATE), jnp.float32),
    )
    state_in = entering((passing, state_end), "row", chain_states, identity)[1]
    y_carried, inflow_pull = jax.vjp(inflow_part, c_float, dt_raw, dt_bias_own, a_log_own, state_in)
    y_flat = (y_local + y_carried).reshape(tok_row, ssm_width)
    gated = y_flat * silu_value(z_gate)
    mix = jnp.concatenate([attended, gated], 1).astype(jnp.bfloat16)
    mix_g = gather_row(mix)
    hidden_one = xf + sum_col(rows_times(mix_g, w_mix_out, False), tok_col)
    scale_two = lax.rsqrt(row_total(jnp.sum(hidden_one * hidden_one, 1)) / D + norm_eps)
    normed_two = hidden_one * scale_two[:, None]
    act_two = (normed_two * gain_two).astype(jnp.bfloat16)
    act_two_g = gather_col(act_two)
    gate_up = sum_row(rows_times(act_two_g, w_gate_up, False), tok_row)
    gate = gate_up[:, :ff_width]
    upper = gate_up[:, ff_width:]
    inner = (silu_value(gate) * upper).astype(jnp.bfloat16)
    inner_g = gather_row(inner)
    y_out = (hidden_one + sum_col(rows_times(inner_g, w_down, False), tok_col)).astype(jnp.bfloat16)
    grad_out_g = gather_col(cotangent)
    grad_inner = sum_row(rows_times(grad_out_g, w_down, True), tok_row)
    grad_down_w = lax.dot_general(
        inner_g, grad_out_g, (((0,), (0,)), ((), ())), preferred_element_type=jnp.float32
    )
    grad_gu = jnp.concatenate(
        [grad_inner * upper * silu_slope(gate), grad_inner * silu_value(gate)], 1
    ).astype(jnp.bfloat16)
    grad_gu_g = gather_row(grad_gu)
    grad_act_two = sum_col(rows_times(grad_gu_g, w_gate_up, True), tok_col)
    grad_gu_w = lax.dot_general(
        act_two_g, grad_gu_g, (((0,), (0,)), ((), ())), preferred_element_type=jnp.float32
    )
    grad_norm_two, gain_two_part = norm_back(grad_act_two, normed_two, scale_two, gain_two)
    grad_hidden = cotangent.astype(jnp.float32) + grad_norm_two
    grad_hidden_g = gather_col(grad_hidden.astype(jnp.bfloat16))
    grad_mix = sum_row(rows_times(grad_hidden_g, w_mix_out, True), tok_row)
    grad_mix_w = lax.dot_general(
        mix_g, grad_hidden_g, (((0,), (0,)), ((), ())), preferred_element_type=jnp.float32
    )
    grad_mix_b = grad_mix.astype(jnp.bfloat16)
    grad_attended = grad_mix_b[:, :q_width].reshape(tok_row, q_local, HD)
    grad_gated = grad_mix_b[:, q_width:].astype(jnp.float32)
    grad_y = (grad_gated * silu_value(z_gate)).reshape(tok_row, head_count, SP)
    grad_z = grad_gated * y_flat * silu_slope(z_gate)
    grad_c_two, grad_dt_two, grad_bias_two, grad_alog_two, grad_state_in = inflow_pull(grad_y)
    adjoint = carried_in((passing, grad_state_in), "row", chain_states, identity)[1]
    grad_passing = jnp.sum(adjoint * state_in, axis=(1, 2))
    grad_x, grad_b, grad_c_one, grad_dt_one, grad_bias_one, grad_alog_one, grad_skip = scan_pull(
        (grad_y, grad_passing, adjoint)
    )
    probs = jnp.exp(attn_scores() - log_total)
    grad_probs = jnp.einsum(
        "qhd,kd->hqk", grad_attended, val_all, preferred_element_type=jnp.float32
    )
    grad_val = jnp.einsum("hqk,qhd->kd", probs_b, grad_attended, preferred_element_type=jnp.float32)
    row_dot = jnp.sum(probs * grad_probs, -1, keepdims=True)
    grad_scores = (probs * (grad_probs - row_dot)).astype(jnp.bfloat16)
    grad_q = (
        jnp.einsum("hqk,kd->qhd", grad_scores, key_all, preferred_element_type=jnp.float32)
        * score_scale
    )
    grad_key = (
        jnp.einsum("hqk,qhd->kd", grad_scores, q_heads, preferred_element_type=jnp.float32)
        * score_scale
    )
    key_total, val_total = (
        lax.psum_scatter(
            grad_key.astype(jnp.bfloat16), "row", scatter_dimension=0, tiled=True
        ).astype(jnp.float32),
        lax.psum_scatter(
            grad_val.astype(jnp.bfloat16), "row", scatter_dimension=0, tiled=True
        ).astype(jnp.float32),
    )
    zero_kv = jnp.zeros((tok_row, KVH * HD), jnp.float32)
    keys_full = lax.dynamic_update_slice(zero_kv, key_total, (0, kv_head * HD))
    vals_full = lax.dynamic_update_slice(zero_kv, val_total, (0, kv_head * HD))
    feature_term = jnp.stack([keys_full, vals_full, grad_b, grad_c_one + grad_c_two], 1)
    feature_term = (
        feature_term.reshape(tok_row, 4, n_col, sub_width)
        .transpose(0, 2, 1, 3)
        .reshape(tok_row, n_col * shared_width)
    )
    grad_shared = lax.psum_scatter(
        feature_term.astype(jnp.bfloat16), "col", scatter_dimension=1, tiled=True
    ).astype(jnp.float32)
    grad_b_pre = grad_shared[:, 2 * sub_width : 3 * sub_width] * silu_slope(b_pre)
    grad_c_pre = grad_shared[:, 3 * sub_width :] * silu_slope(c_pre)
    grad_x_pre = grad_x.reshape(tok_row, ssm_width) * silu_slope(x_pre)
    grad_proj = jnp.concatenate(
        [
            grad_q.reshape(tok_row, q_width),
            grad_shared[:, : 2 * sub_width],
            grad_b_pre,
            grad_c_pre,
            grad_z,
            grad_x_pre,
            grad_dt_one + grad_dt_two,
        ],
        1,
    ).astype(jnp.bfloat16)
    rounded_own = grad_proj.astype(jnp.float32)
    cbias_bc_grad = jnp.sum(rounded_own[:, col_b:col_z], 0)
    cbias_x_grad = jnp.sum(rounded_own[:, col_x:col_dt], 0)
    grad_proj_g = gather_row(grad_proj)
    grad_bc_rows = grad_proj_g[:, col_b:col_z].astype(jnp.float32)
    grad_x_rows = grad_proj_g[:, col_x:col_dt].astype(jnp.float32)
    pad_bc = jnp.zeros((CONV - 1, grad_bc_rows.shape[1]), jnp.float32)
    pad_x = jnp.zeros((CONV - 1, grad_x_rows.shape[1]), jnp.float32)
    raw_bc = conv_back(jnp.concatenate([grad_bc_rows, pad_bc], 0), seg_pad_bottom, kern_bc, SEQ)
    raw_x = conv_back(jnp.concatenate([grad_x_rows, pad_x], 0), seg_pad_bottom, kern_x, SEQ)
    grad_raw = jnp.concatenate(
        [
            grad_proj_g[:, :col_b],
            raw_bc.astype(jnp.bfloat16),
            grad_proj_g[:, col_z:col_x],
            raw_x.astype(jnp.bfloat16),
            grad_proj_g[:, col_dt:],
        ],
        1,
    )
    pre_bc = jnp.dot(act_one_g, w_mix_in[:, col_b:col_z], preferred_element_type=jnp.float32)
    pre_x = jnp.dot(act_one_g, w_mix_in[:, col_x:col_dt], preferred_element_type=jnp.float32)
    kern_bc_grad = kernel_grad(grad_bc_rows, jnp.concatenate([pad_bc, pre_bc], 0), seg_pad_top)
    kern_x_grad = kernel_grad(grad_x_rows, jnp.concatenate([pad_x, pre_x], 0), seg_pad_top)
    grad_in_w = lax.dot_general(
        act_one_g, grad_raw, (((0,), (0,)), ((), ())), preferred_element_type=jnp.float32
    )
    grad_act_one = sum_col(rows_times(grad_raw, w_mix_in, True), tok_col)
    grad_norm_one, gain_one_part = norm_back(grad_act_one, normed_one, scale_one, gain_one)
    x_grad = (grad_hidden + grad_norm_one).astype(jnp.bfloat16)
    contrib = jnp.zeros((small_params.shape[0],), jnp.float32)
    contrib = lax.dynamic_update_slice(contrib, gain_one_part, (row_index * width_row,))
    contrib = lax.dynamic_update_slice(contrib, gain_two_part, (D + row_index * width_row,))
    contrib = lax.dynamic_update_slice(
        contrib, grad_alog_one + grad_alog_two, (off_alog + col_index * head_count,)
    )
    contrib = lax.dynamic_update_slice(
        contrib, grad_bias_one + grad_bias_two, (off_dtb + col_index * head_count,)
    )
    contrib = lax.dynamic_update_slice(contrib, grad_skip, (off_skip + col_index * head_count,))
    kern_table = jnp.zeros((CONV, conv_width), jnp.float32)
    kern_table = lax.dynamic_update_slice(kern_table, kern_x_grad, (0, col_index * ssm_width))
    kern_table = lax.dynamic_update_slice(
        kern_table, kern_bc_grad[:, :sub_width], (0, SH * SP + col_index * sub_width)
    )
    kern_table = lax.dynamic_update_slice(
        kern_table, kern_bc_grad[:, sub_width:], (0, SH * SP + STATE + col_index * sub_width)
    )
    contrib = lax.dynamic_update_slice(contrib, kern_table.reshape(-1), (off_kern,))
    bias_table = jnp.zeros((conv_width,), jnp.float32)
    bias_table = lax.dynamic_update_slice(bias_table, cbias_x_grad, (col_index * ssm_width,))
    bias_table = lax.dynamic_update_slice(
        bias_table, cbias_bc_grad[:sub_width], (SH * SP + col_index * sub_width,)
    )
    bias_table = lax.dynamic_update_slice(
        bias_table, cbias_bc_grad[sub_width:], (SH * SP + STATE + col_index * sub_width,)
    )
    contrib = lax.dynamic_update_slice(contrib, bias_table, (off_cbias,))
    small_grad = lax.psum(contrib, ("dp", "row", "col"))
    small_moment, small_second, small_update = adam_step(small_grad, small_m, small_v, small_params)
    weights_local = (w_mix_in, w_mix_out, w_gate_up, w_down)
    group_size = n_dp // OWNERS
    piece_len = mat_m.shape[-1]
    capacity = piece_len * group_size
    my_group = dp_index // group_size
    my_piece = dp_index % group_size
    slot_len = max(
        max(width_row * w_mix_in.shape[1], mix_width * width_row),
        max(width_row * 2 * ff_width, ff_width * width_row),
    )
    offsets = []
    for matrix_index in range(MATS):
        earlier = jnp.int32(0)
        for other_index in range(matrix_index):
            earlier = earlier + (owner[other_index] == owner[matrix_index]).astype(jnp.int32)
        offsets.append(earlier * slot_len)

    def place(buffer, block_values, matrix_index):
        updated = lax.dynamic_update_slice(
            buffer, block_values.reshape(-1), (offsets[matrix_index],)
        )
        return jnp.where(owner[matrix_index] == my_group, updated, buffer)

    def own_piece(buffer):
        return lax.dynamic_slice_in_dim(buffer, my_piece * piece_len, piece_len)

    weight_buffer = jnp.zeros((capacity,), jnp.float32)
    for matrix_index in range(MATS):
        weight_buffer = place(
            weight_buffer, weights_local[matrix_index].astype(jnp.float32), matrix_index
        )
    weight_piece = own_piece(weight_buffer)
    totals = (
        lax.psum(grad_in_w.astype(jnp.bfloat16), "dp").astype(jnp.float32),
        lax.psum(grad_mix_w.astype(jnp.bfloat16), "dp").astype(jnp.float32),
        lax.psum(grad_gu_w.astype(jnp.bfloat16), "dp").astype(jnp.float32),
        lax.psum(grad_down_w.astype(jnp.bfloat16), "dp").astype(jnp.float32),
    )
    grad_buffer = jnp.zeros((capacity,), jnp.float32)
    for matrix_index in range(MATS):
        grad_buffer = place(grad_buffer, totals[matrix_index], matrix_index)
    grad_piece = own_piece(grad_buffer)
    moment_new, second_new, update = adam_step(
        grad_piece, mat_m.reshape(piece_len), mat_v.reshape(piece_len), weight_piece
    )
    fresh_piece = (weight_piece + update).astype(jnp.bfloat16)
    fresh_all = lax.all_gather(fresh_piece, "dp", axis=0, tiled=True)
    new_weights = []
    for matrix_index in range(MATS):
        shape_here = weights_local[matrix_index].shape
        start_here = owner[matrix_index] * capacity + offsets[matrix_index]
        new_weights.append(
            lax.dynamic_slice_in_dim(fresh_all, start_here, shape_here[0] * shape_here[1]).reshape(
                shape_here
            )
        )
    out_shape = (1, 1, 1, piece_len)
    return (
        y_out,
        x_grad,
        grad_piece.reshape(out_shape),
        moment_new.reshape(out_shape),
        second_new.reshape(out_shape),
        update.reshape(out_shape),
        new_weights[0],
        new_weights[1],
        new_weights[2],
        new_weights[3],
        small_grad,
        small_moment,
        small_second,
        small_update,
    )


def solution(mesh):
    placed = (
        P(("dp", "col"), "row"),
        P(("dp", "col"), "row"),
        P("dp", None),
        P(),
        P("row", "col"),
        P("col", "row"),
        P("row", "col"),
        P("col", "row"),
        P("row", "col", "dp", None),
        P("row", "col", "dp", None),
        P(),
        P(),
        P(),
    )
    return jax.shard_map(
        shards,
        mesh=mesh,
        in_specs=placed,
        out_specs=(
            P(("dp", "col"), "row"),
            P(("dp", "col"), "row"),
            P("row", "col", "dp", None),
            P("row", "col", "dp", None),
            P("row", "col", "dp", None),
            P("row", "col", "dp", None),
            P("row", "col"),
            P("col", "row"),
            P("row", "col"),
            P("col", "row"),
            P(),
            P(),
            P(),
            P(),
        ),
        check_vma=False,
    )
```

profile of v0, /device:TPU:0, one launch (start us, length us, event | category | flops | bytes accessed | tf_op | source)
XLA Modules:
  0.0 1977.0 jit_solution(3744610191815288132)
XLA Ops:
  18.1 45.4 %all-gather.16.cloned.1.call-done = bf16[1024,1024]{1,0:T(8,128)(2,1)} async-done(((bf16[256,1024]{1,0:T(8,128)(2,1)}), bf16[1024,1024]{1,0:T(8,128)(2,1)}) %all-gather.16.cloned.1.call-update) | async-done | bytes 2097168 | tf_op jit(solution)/shard_map/all_gather | solution.py:95
  119.9 11.7 all-gather.18.cloned.1.call-done
  142.3 193.9 %while.114 = (s32[]{:T(128)}, f32[12,64,256]{2,1,0:T(8,128)S(1)}, s32[]{:T(128)}, f32[4,128,12,64]{1,0,3,2:T(4,128)}, pred[4,128,128,12]{2,1,3,0:T(32,128)(4,1)}...) while((s32[]{:T(128)}, f32[12,64,256]{2,1,0:T(8,128)S(1)}, ...), condition=%wide.region_7.9_spmd.clone, body=%wide.region_5.8_spmd.clone.sunk | while | flops 808904704 | bytes 12390637 | solution.py:214
  174.5 10.7 dynamic_update_slice.378
  223.1 10.7 dynamic_update_slice.378
  271.5 10.7 dynamic_update_slice.378
  320.0 10.7 dynamic_update_slice.378
  352.8 10.7 all-gather.20.cloned.1.call-done
  370.2 77.5 %reduce-scatter.14.cloned.1.call-done = f32[256,1024]{1,0:T(8,128)} async-done(((f32[1024,1024]{1,0:T(8,128)}), f32[256,1024]{1,0:T(8,128)}) %reduce-scatter.14.cloned.1.call-update) | async-done | bytes 1048592 | tf_op jit(solution)/shard_map/reduce_scatter | solution.py:112
  452.6 42.7 %all-gather.26.cloned.1.call-done = bf16[1024,1024]{1,0:T(8,128)(2,1)} async-done(((bf16[256,1024]{1,0:T(8,128)(2,1)}), bf16[1024,1024]{1,0:T(8,128)(2,1)}) %all-gather.26.cloned.1.call-update) | async-done | bytes 2097168 | tf_op jit(solution)/shard_map/all_gather | solution.py:95
  502.0 40.0 %all-gather.22.cloned.1.call-done = bf16[1024,1024]{1,0:T(8,128)(2,1)} async-done(((bf16[256,1024]{1,0:T(8,128)(2,1)}), bf16[1024,1024]{1,0:T(8,128)(2,1)}) %all-gather.22.cloned.1.call-update) | async-done | bytes 2097168 | tf_op jit(solution)/shard_map/all_gather | solution.py:95
  541.9 11.2 fusion.251
  555.7 20.6 %reduce-scatter.16.cloned.1.call-done = f32[512,2048]{1,0:T(8,128)} async-done(((f32[1024,2048]{1,0:T(8,128)}), f32[512,2048]{1,0:T(8,128)}) %reduce-scatter.16.cloned.1.call-update) | async-done | bytes 4194320 | tf_op jit(solution)/shard_map/reduce_scatter | solution.py:99
  583.2 14.9 all-gather.28.cloned.1.call-done
  608.2 78.1 %reduce-scatter.22.cloned.1.call-done = f32[256,1024]{1,0:T(8,128)} async-done(((f32[1024,1024]{1,0:T(8,128)}), f32[256,1024]{1,0:T(8,128)}) %reduce-scatter.22.cloned.1.call-update) | async-done | bytes 1048592 | tf_op jit(solution)/shard_map/reduce_scatter | solution.py:112
  693.3 46.3 %all-gather.30.cloned.1.call-done = bf16[1024,1024]{1,0:T(8,128)(2,1)} async-done(((bf16[256,1024]{1,0:T(8,128)(2,1)}), bf16[1024,1024]{1,0:T(8,128)(2,1)}) %all-gather.30.cloned.1.call-update) | async-done | bytes 2097168 | tf_op jit(solution)/shard_map/all_gather | solution.py:95
  747.0 10.0 reduce-scatter.24.cloned.1.call-done
  788.9 219.7 %while.116 = (s32[]{:T(128)}, f32[12]{0:T(128)}, f32[12,64,256]{2,1,0:T(8,128)S(1)}, f32[4,128,12,64]{1,0,3,2:T(4,128)}, bf16[4,128,256]{2,1,0:T(8,128)(2,1)}, /...) while((s32[]{:T(128)}, f32[12]{0:T(128)}, ...), condition=%wide.region_38.40_spmd.clone, body=%wide.region_28.39_spmd.clone.sunk | while | flops 1614317568 | bytes 23147580 | solution.py:214
  833.0 10.7 dynamic_update_slice.384
  888.0 10.7 dynamic_update_slice.384
  942.9 10.7 dynamic_update_slice.384
  997.9 10.7 dynamic_update_slice.384
  1030.2 15.4 reduce-scatter.30.cloned.1.call-done
  1059.1 11.7 all-gather.32.cloned.1.call-done
  1125.7 10.9 reshape.841
  1144.3 20.8 %broadcast_multiply_fusion.3 = f32[1,1,1,4218880]{3,2,1,0:T(1,128)} fusion(f32[1,1,1,4218880]{3,2,1,0:T(1,128)} %param.31), kind=kLoop, calls=%fused_computation.177 | loop fusion | flops 4218880 | bytes 33751040 | tf_op jit(solution)/shard_map/mul | solution.py:87
  1189.7 11.0 reshape.852
  1237.1 178.2 %all-reduce.18.cloned.1.call-done = (bf16[2109440]{0:T(1024)(128)(2,1)}, bf16[1048576]{0:T(1024)(128)(2,1)}, bf16[2097152]{0:T(1024)(128)(2,1)}, bf16[1048576]{0:T(1024)(128)(2,1)}) async-done(((bf16[2109440]{0:T(1024)(128)(2,1)}, bf16[1048576]{0:T(1024)(128)(2,1)}, bf16[2097152]{0:T(1024)(128)(2,1)}, bf16[1048576]{0:T(1024)(128)(2,1)}), (bf16[2109440]{0:T(1024)(128)(2,1)}, bf16[1048576]{0:T(1024)(128)(2,1)}, ...) | async-done | bytes 12607504 | tf_op jit(solution)/shard_map/psum | solution.py:595
  1415.3 15.1 convert_select_fusion
  1466.5 45.5 %add_convert_fusion = (bf16[4218880]{0:T(1024)(128)(2,1)}, f32[4218880]{0:T(1024)}, f32[4218880]{0:T(1024)}, f32[4218880]{0:T(1024)}) fusion(f32[4218880]{0:T(1024)} %select_dynamic-update-slice_fusion.2, f32[4218880]{0:T(1024)} %bitcast.628, f32[4218880]{0:T(1024)} %select_dynamic-update-slice_fusion.4, f32[4218880]{0:T(1024)} %bitcast.634), kind=kLoop, calls=%fused_computation.173 | loop fusion | flops 59064320 | bytes 126566400 | tf_op jit(solution)/shard_map/convert_element_type | solution.py:607
  1520.6 103.7 %all-reduce.16.cloned.1.call-done = f32[22160]{0:T(1024)} async-done(((f32[22160]{0:T(1024)}), f32[22160]{0:T(1024)}) %all-reduce.16.cloned.1.call-update) | async-done | bytes 88656 | tf_op jit(solution)/shard_map/psum | solution.py:560
  1625.9 301.7 %all-gather.34.cloned.1.call-done = bf16[16875520]{0:T(1024)(128)(2,1)} async-done(((bf16[4218880]{0:T(1024)(128)(2,1)}), bf16[16875520]{0:T(1024)(128)(2,1)}) %all-gather.34.cloned.1.call-update) | async-done | bytes 33751056 | tf_op jit(solution)/shard_map/all_gather | solution.py:608
  (865 shorter events, 733.9 us)
Async XLA Ops:
  7.2 56.3 %all-gather.16.cloned.1.call-start = ((), (), s32[]{:S(2)}) async-start(), calls=%async_computation.11 | async-start | bytes 2621440 | tf_op jit(solution)/shard_map/all_gather | solution.py:95
  15.1 82.7 %reduce-scatter.12.cloned.1.call-start = ((), (), s32[]{:S(2)}) async-start(), calls=%async_computation.12 | async-start | bytes 12681216 | tf_op jit(solution)/shard_map/reduce_scatter | solution.py:99
  16.2 61.0 %copy-start.71 = (f32[768]{0:T(1024)}, f32[768]{0:T(1024)S(1)}, u32[]{:S(2)}) copy-start(f32[768]{0:T(1024)S(1)} %get-tuple-element.1961) | copy-start | bytes 9220
  16.3 61.0 %copy-start.73 = (f32[768]{0:T(1024)}, f32[768]{0:T(1024)S(1)}, u32[]{:S(2)}) copy-start(f32[768]{0:T(1024)S(1)} %get-tuple-element.1962) | copy-start | bytes 9220
  82.4 49.2 %all-gather.18.cloned.1.call-start = ((), (), s32[]{:S(2)}) async-start(), calls=%async_computation.13 | async-start | bytes 1310720 | tf_op jit(solution)/shard_map/all_gather | solution.py:338
  102.2 261.3 %all-gather.20.cloned.1.call-start = ((), (), s32[]{:S(2)}) async-start(), calls=%async_computation.14 | async-start | bytes 3145728 | tf_op jit(solution)/shard_map/all_gather | solution.py:108
  352.4 95.3 %reduce-scatter.14.cloned.1.call-start = ((), (), s32[]{:S(2)}) async-start(), calls=%async_computation.15 | async-start | bytes 5242880 | tf_op jit(solution)/shard_map/reduce_scatter | solution.py:112
  369.5 78.2 %copy-start.16 = (bf16[256,1024]{1,0:T(8,128)(2,1)S(1)}, bf16[256,1024]{1,0:T(8,128)(2,1)}, u32[]{:S(2)}) copy-start(bf16[256,1024]{1,0:T(8,128)(2,1)} %param.22) | copy-start | bytes 1572868
  369.5 82.1 %copy-start.56 = (f32[1024]{0:T(1024)S(1)}, f32[1024]{0:T(1024)}, u32[]{:S(2)}) copy-start(f32[1024]{0:T(1024)} %get-tuple-element.2185) | copy-start | bytes 12292
  369.5 125.8 %all-gather.26.cloned.1.call-start = ((), (), s32[]{:S(2)}) async-start(), calls=%async_computation.20 | async-start | bytes 2621440 | tf_op jit(solution)/shard_map/all_gather | solution.py:95
  370.1 171.8 %all-gather.22.cloned.1.call-start = ((), (), s32[]{:S(2)}) async-start(), calls=%async_computation.16 | async-start | bytes 2621440 | tf_op jit(solution)/shard_map/all_gather | solution.py:95
  449.1 241.8 %copy-start.5 = (f32[256,1024]{1,0:T(8,128)}, f32[256,1024]{1,0:T(8,128)S(1)}, u32[]{:S(2)}) copy-start(f32[256,1024]{1,0:T(8,128)S(1)} %get-tuple-element.2135) | copy-start | bytes 3145732
  451.6 239.3 %copy-start.83 = (f32[256]{0:T(256)}, f32[256]{0:T(256)S(1)}, u32[]{:S(2)}) copy-start(f32[256]{0:T(256)S(1)} %add_rsqrt_fusion) | copy-start | bytes 3076
  452.6 103.1 %reduce-scatter.20.cloned.1.call-start = ((), (), s32[]{:S(2)}) async-start(), calls=%async_computation.21 | async-start | bytes 6291456 | tf_op jit(solution)/shard_map/reduce_scatter | solution.py:99
  501.9 74.3 %reduce-scatter.16.cloned.1.call-start = ((), (), s32[]{:S(2)}) async-start(), calls=%async_computation.17 | async-start | bytes 12582912 | tf_op jit(solution)/shard_map/reduce_scatter | solution.py:99
  553.2 44.9 %all-gather.28.cloned.1.call-start = ((), (), s32[]{:S(2)}) async-start(), calls=%async_computation.22 | async-start | bytes 6291456 | tf_op jit(solution)/shard_map/all_gather | solution.py:108
  583.0 103.3 %reduce-scatter.22.cloned.1.call-start = ((), (), s32[]{:S(2)}) async-start(), calls=%async_computation.23 | async-start | bytes 5242880 | tf_op jit(solution)/shard_map/reduce_scatter | solution.py:112
  608.1 82.8 %copy-start.25 = (bf16[256,1024]{1,0:T(8,128)(2,1)S(1)}, bf16[256,1024]{1,0:T(8,128)(2,1)}, u32[]{:S(2)}) copy-start(bf16[256,1024]{1,0:T(8,128)(2,1)} %param.23) | copy-start | bytes 1572868
  608.1 131.4 %all-gather.30.cloned.1.call-start = ((), (), s32[]{:S(2)}) async-start(), calls=%async_computation.24 | async-start | bytes 2621440 | tf_op jit(solution)/shard_map/all_gather | solution.py:95
  693.3 63.8 %reduce-scatter.24.cloned.1.call-start = ((), (), s32[]{:S(2)}) async-start(), calls=%async_computation.25 | async-start | bytes 6291456 | tf_op jit(solution)/shard_map/reduce_scatter | solution.py:99
  746.2 267.2 %reduce-scatter.28.cloned.1.call-start = ((), (), s32[]{:S(2)}) async-start(), calls=%async_computation.27 | async-start | bytes 393216 | tf_op jit(solution)/shard_map/reduce_scatter | solution.py:471
  760.7 253.8 %reduce-scatter.26.cloned.1.call-start = ((), (), s32[]{:S(2)}) async-start(), calls=%async_computation.26 | async-start | bytes 393216 | tf_op jit(solution)/shard_map/reduce_scatter | solution.py:468
  785.8 259.8 %reduce-scatter.30.cloned.1.call-start = ((), (), s32[]{:S(2)}) async-start(), calls=%async_computation.28 | async-start | bytes 1310720 | tf_op jit(solution)/shard_map/reduce_scatter | solution.py:484
  1016.9 54.0 %all-gather.32.cloned.1.call-start = ((), (), s32[]{:S(2)}) async-start(), calls=%async_computation.29 | async-start | bytes 6340608 | tf_op jit(solution)/shard_map/all_gather | solution.py:108
  1058.5 32.9 %all-gather.24.cloned.1.call-start = ((), (), s32[]{:S(2)}) async-start(), calls=%async_computation.18 | async-start | bytes 3145728 | tf_op jit(solution)/shard_map/all_gather | solution.py:108
  1059.1 174.3 %reduce-scatter.32.cloned.1.call-start = ((), (), s32[]{:S(2)}) async-start(), calls=%async_computation.30 | async-start | bytes 5242880 | tf_op jit(solution)/shard_map/reduce_scatter | solution.py:112
  1091.3 324.0 %all-reduce.18.cloned.1.call-start = ((), (), s32[]{:S(2)}) async-start(), calls=%async_computation.33 | async-start | bytes 25214976 | tf_op jit(solution)/shard_map/psum | solution.py:595
  1136.6 380.9 %reduce-scatter.18.cloned.1.call-start = ((), (), s32[]{:S(2)}) async-start(), calls=%async_computation.19 | async-start | bytes 5242880 | tf_op jit(solution)/shard_map/reduce_scatter | solution.py:112
  1144.2 480.1 %all-reduce.16.cloned.1.call-start = ((), (), s32[]{:S(2)}) async-start(), calls=%async_computation.32 | async-start | bytes 180224 | tf_op jit(solution)/shard_map/psum | solution.py:560
  1237.0 690.6 %all-gather.34.cloned.1.call-start = ((), (), s32[]{:S(2)}) async-start(), calls=%async_computation.31 | async-start | bytes 42188800 | tf_op jit(solution)/shard_map/all_gather | solution.py:608
  1517.5 106.8 %copy-start.64 = (f32[22160]{0:T(1024)S(1)}, f32[22160]{0:T(1024)}, u32[]{:S(2)}) copy-start(f32[22160]{0:T(1024)} %param.33) | copy-start | bytes 265924
  1517.5 106.8 %copy-start.65 = (f32[22160]{0:T(1024)S(1)}, f32[22160]{0:T(1024)}, u32[]{:S(2)}) copy-start(f32[22160]{0:T(1024)} %param.34) | copy-start | bytes 265924
  (134 other events, 1677.4 us)
Sparse Core Ops, SparseCore 0:
  15.2 48.2 all-gather.15
  82.6 15.2 reduce-scatter.11
  102.3 29.2 all-gather.17
  352.5 10.9 all-gather.19
  369.7 77.9 reduce-scatter.13
  449.1 46.1 all-gather.25
  497.4 44.4 all-gather.21
  544.8 10.8 reduce-scatter.19
  558.5 17.6 reduce-scatter.15
  583.1 14.9 all-gather.27
  608.3 77.9 reduce-scatter.21
  693.4 46.1 all-gather.29
  746.3 10.6 reduce-scatter.23
  760.8 8.9 reduce-scatter.27
  786.0 9.0 reduce-scatter.25
  1017.0 28.5 reduce-scatter.29
  1058.6 12.2 all-gather.31
  1072.8 11.7 all-gather.23
  1091.4 77.9 reduce-scatter.31
  1174.4 240.8 all-reduce.17
  1417.6 77.9 reduce-scatter.17
  1501.7 122.5 all-reduce.15
  1626.2 301.4 all-gather.33
where the time goes:
time: 1990 us; the launch traced here: 1980 us
  waiting for transfers between devices  1020 us (51%)
  local copies, waits for them, and re-layouts  353 us (18%)
  other arithmetic  336 us (17%)
  matrix products  207 us (10%)
  between operations  31.4 us (2%)
  blocking collectives  22.1 us (1%)
    all_gather x1, waiting for transfers between devices, shards(): fresh_all = lax.all_gather(fresh_piece, 'dp', axis=0, tiled=True)  302 us
    psum x1, waiting for transfers between devices, shards(): lax.psum(grad_in_w.astype(jnp.bfloat16), 'dp').astype(jnp.float32)  178 us
    all_gather x4, waiting for transfers between devices, gather_col(): return lax.all_gather(values, 'col', axis=0, tiled=True)  174 us
    reduce_scatter x4, waiting for transfers between devices, sum_col(): lax.psum_scatter(term_fn(jnp.int32(0), row_total_count * lax.axis_size('c...  156 us
    dynamic_update_slice x56, local copies, waits for them, and re-layouts, scan_blocks(): lax.scan(one_block, (start_state, prev_seg), inputs)  124 us
    psum x1, waiting for transfers between devices, shards(): small_grad = lax.psum(contrib, ('dp', 'row', 'col'))  104 us
    unnamed x266, local copies, waits for them, and re-layouts  63.8 us
    select_n x7, other arithmetic, place(): return jnp.where(owner[matrix_index] == my_group, updated, buffer)  50.8 us
  transfers between devices with their start and end apart: 23, of which 18 were waited for; matrix products, arithmetic and copies ran while one was open for 28% of the time, Pallas kernels for 0%

commit v1 on v0

v1 whole, which is shorter than its diff:
```python
import functools

import jax
import jax.numpy as jnp
from jax import lax
from jax.experimental import pallas as pl
from jax.experimental.pallas import tpu as pltpu
from jax.sharding import PartitionSpec as P

D = 2048
FF = 4096
QH = 8
KVH = 2
HD = 128
SH = 48
SP = 64
STATE = 256
CONV = 4
SPAN = 128
SEQ = 1024
MATS = 4
OWNERS = 4
STEP = 4
LANES = 128

highest = lax.Precision.HIGHEST
norm_eps = 1e-05
beta_one = 0.5
beta_two = 0.6
learn_rate = 0.02
adam_eps = 1e-08
weight_decay = 0.1
masked_score = -1e30
NN = ((1,), (0,))
NT = ((1,), (1,))
TN = ((0,), (0,))
bf16 = jnp.bfloat16
f32 = jnp.float32


def mm(left, right, dims, precision=None):
    return lax.dot_general(
        left, right, (dims, ((), ())), preferred_element_type=f32, precision=precision
    )


def silu_value(values):
    return values * jax.nn.sigmoid(values)


def silu_slope(values):
    sigmoid = jax.nn.sigmoid(values)
    return sigmoid * (1.0 + values * (1.0 - sigmoid))


def adam_step(gradient, moment, second, weight):
    moment_new = beta_one * moment + (1.0 - beta_one) * gradient
    second_new = beta_two * second + (1.0 - beta_two) * gradient * gradient
    first_hat = moment_new / (1.0 - beta_one**STEP)
    second_hat = second_new / (1.0 - beta_two**STEP)
    update = -learn_rate * (first_hat / (jnp.sqrt(second_hat) + adam_eps) + weight_decay * weight)
    return (moment_new, second_new, update)


def head_table(heads):
    rows = lax.broadcasted_iota(jnp.int32, (8, heads * SP), 0)
    cols = lax.broadcasted_iota(jnp.int32, (8, heads * SP), 1)
    return (cols // SP == rows).astype(f32)


def head_table_t(heads):
    rows = lax.broadcasted_iota(jnp.int32, (heads * SP, 8), 0)
    cols = lax.broadcasted_iota(jnp.int32, (heads * SP, 8), 1)
    return (rows // SP == cols).astype(f32)


def block_rows(block):
    return pl.ds(pl.multiple_of(block * SPAN, SPAN), SPAN)


def decay_parts(block, a_ref, at_ref, dt_ref, meta_ref, segc_ref, segr_ref, table):
    rows = block_rows(block)
    t_pos = lax.broadcasted_iota(jnp.int32, (SPAN, SPAN), 0)
    s_pos = lax.broadcasted_iota(jnp.int32, (SPAN, SPAN), 1)
    lower = t_pos >= s_pos
    upper = (t_pos <= s_pos).astype(f32)
    run = mm(lower.astype(f32), a_ref[rows, :], NN, highest)
    run_t = mm(at_ref[:, rows], upper, NN, highest)
    live = (segc_ref[rows, :] == segr_ref[:, rows]) & lower
    meta = meta_ref[rows, :]
    same_prev, same_last = meta[:, 0:1], meta[:, 1:2]
    run_last = run[SPAN - 1 : SPAN, :]
    enter = jnp.exp(run) * same_prev
    leave = jnp.exp(run_last - run) * same_last
    passing = jnp.exp(run_last) * same_prev[SPAN - 1 : SPAN, :]
    wide = mm(jnp.concatenate([dt_ref[rows, :], enter, leave], 0), table, NN, highest)
    return rows, run, run_t, live, passing, wide[:SPAN], wide[SPAN : 2 * SPAN], wide[2 * SPAN :]


def decay_of(run, run_t, live, head):
    logs = run[:, head : head + 1] - run_t[head : head + 1, :]
    return jnp.where(live, jnp.exp(jnp.where(live, logs, 0.0)), 0.0)


def mixer_forward_kernel(
    heads, q_heads, q_ref, k_ref, v_ref, xs_ref, z_ref, bm_ref, cm_ref, dt_ref, a_ref, at_ref,
    meta_ref, segc_ref, segr_ref, skip_ref, mix_ref, y_ref, st_ref, state,
):
    q_width = q_heads * HD
    tokens = xs_ref.shape[0]
    table = head_table(heads)
    table_t = head_table_t(heads)
    state[...] = jnp.zeros_like(state)

    def one(block, carry):
        rows, run, run_t, live, passing, dt_w, enter_w, leave_w = decay_parts(
            block, a_ref, at_ref, dt_ref, meta_ref, segc_ref, segr_ref, table
        )
        b_blk, c_blk = bm_ref[rows, :], cm_ref[rows, :]
        x_blk = xs_ref[rows, :].astype(f32)
        inflow = dt_w * x_blk
        inflow_b = inflow.astype(bf16)
        old = state[...]
        st_ref[block] = old
        inter = mm(c_blk, b_blk, NT)
        y_in = enter_w * mm(c_blk, old.astype(bf16), NT)
        parts = []
        for head in range(heads):
            table_h = (decay_of(run, run_t, live, head) * inter).astype(bf16)
            parts.append(mm(table_h, inflow_b[:, head * SP : (head + 1) * SP], NN))
        y_blk = jnp.concatenate(parts, 1) + y_in + skip_ref[...] * x_blk
        y_ref[rows, :] = y_blk
        mix_ref[rows, q_width:] = (y_blk * silu_value(z_ref[rows, :])).astype(bf16)
        pass_col = jnp.sum(table_t * passing, 1, keepdims=True)
        state[...] = pass_col * old + mm((leave_w * inflow).astype(bf16), b_blk, TN)
        return carry

    lax.fori_loop(0, tokens // SPAN, one, 0)
    chunk = 256
    for first in range(0, tokens, chunk):
        known = first + chunk
        rows = slice(first, known)
        q_pos = first + lax.broadcasted_iota(jnp.int32, (chunk, known), 0)
        k_pos = lax.broadcasted_iota(jnp.int32, (chunk, known), 1)
        allowed = (k_pos <= q_pos) & (segc_ref[rows, :] == segr_ref[:, :known])
        for head in range(q_heads):
            lanes = slice(head * HD, (head + 1) * HD)
            scores = mm(q_ref[rows, lanes], k_ref[:known, :], NT) * HD ** (-0.5)
            scores = jnp.where(allowed, scores, masked_score)
            expo = jnp.exp(scores - jnp.max(scores, 1, keepdims=True))
            probs = (expo / jnp.sum(expo, 1, keepdims=True)).astype(bf16)
            mix_ref[rows, lanes] = mm(probs, v_ref[:known, :], NN).astype(bf16)


def mixer_backward_kernel(
    heads, q_heads, gm_ref, q_ref, k_ref, v_ref, xs_ref, z_ref, y_ref, bm_ref, cm_ref, dt_ref,
    a_ref, at_ref, meta_ref, segc_ref, segr_ref, skip_ref, rate_ref, st_ref,
    gq_ref, gk_ref, gv_ref, gz_ref, gx_ref, gdt_ref, gb_ref, gc_ref, small_ref, gskip_ref,
    grad_state,
):
    q_width = q_heads * HD
    tokens = xs_ref.shape[0]
    blocks = tokens // SPAN
    table = head_table(heads)
    table_t = head_table_t(heads)
    grad_state[...] = jnp.zeros_like(grad_state)
    small_ref[...] = jnp.zeros_like(small_ref)
    gskip_ref[...] = jnp.zeros_like(gskip_ref)
    t_pos = lax.broadcasted_iota(jnp.int32, (SPAN, SPAN), 0)
    s_pos = lax.broadcasted_iota(jnp.int32, (SPAN, SPAN), 1)
    upper = (t_pos <= s_pos).astype(f32)

    def one(step, carry):
        block = blocks - 1 - step
        rows, run, run_t, live, passing, dt_w, enter_w, leave_w = decay_parts(
            block, a_ref, at_ref, dt_ref, meta_ref, segc_ref, segr_ref, table
        )
        b_blk, c_blk = bm_ref[rows, :], cm_ref[rows, :]
        x_blk = xs_ref[rows, :].astype(f32)
        z_blk = z_ref[rows, :]
        grad_gated = gm_ref[rows, q_width:].astype(bf16).astype(f32)
        gy = grad_gated * silu_value(z_blk)
        gz_ref[rows, :] = grad_gated * y_ref[rows, :] * silu_slope(z_blk)
        gy_b = gy.astype(bf16)
        inflow = dt_w * x_blk
        inflow_b = inflow.astype(bf16)
        old = st_ref[block]
        old_b = old.astype(bf16)
        later = grad_state[...]
        later_b = later.astype(bf16)
        enter_gy = (enter_w * gy).astype(bf16)
        leave_in = (leave_w * inflow).astype(bf16)
        from_later = leave_w * mm(b_blk, later_b, NT)
        y_in = enter_w * mm(c_blk, old_b, NT)
        inter = mm(c_blk, b_blk, NT)
        grad_inter = jnp.zeros((SPAN, SPAN), f32)
        parts, row_sums, col_sums = [], [], []
        for head in range(heads):
            lanes = slice(head * SP, (head + 1) * SP)
            decay = decay_of(run, run_t, live, head)
            weight = decay * inter
            cross = mm(gy_b[:, lanes], inflow_b[:, lanes], NT)
            grad_inter = grad_inter + decay * cross
            pairs = weight * cross
            row_sums.append(jnp.sum(pairs, 1, keepdims=True))
            col_sums.append(jnp.sum(pairs, 0, keepdims=True))
            parts.append(mm(weight.astype(bf16), gy_b[:, lanes], TN))
        pad = 8 - heads
        row_sum = jnp.concatenate(row_sums + [jnp.zeros((SPAN, pad), f32)], 1)
        col_sum = jnp.concatenate(col_sums + [jnp.zeros((pad, SPAN), f32)], 0)
        grad_inflow = jnp.concatenate(parts, 1) + from_later
        stacked = jnp.concatenate([gy * y_in, inflow * from_later, grad_inflow * x_blk], 0)
        sums = mm(stacked, table_t, NN, highest)
        row_in, col_in, dt_in = sums[:SPAN], sums[SPAN : 2 * SPAN], sums[2 * SPAN :]
        state_dot = jnp.sum(later * old, 1, keepdims=True)
        state_heads = jnp.sum(table_t * state_dot, 0, keepdims=True)
        tail = passing * state_heads + jnp.sum(col_in, 0, keepdims=True)
        grad_a = (
            mm(upper, row_sum + row_in - col_in, NN, highest)
            - mm(upper, col_sum, NT, highest)
            + tail
        )
        dt_blk = dt_ref[rows, :]
        grad_raw = (grad_a * rate_ref[...] + dt_in) * (1.0 - jnp.exp(-dt_blk))
        gdt_ref[rows, :] = grad_raw
        small_ref[0:1, :] += jnp.sum(grad_a * dt_blk, 0, keepdims=True)
        small_ref[1:2, :] += jnp.sum(grad_raw, 0, keepdims=True)
        gskip_ref[...] += jnp.sum(gy * x_blk, 0, keepdims=True)
        gx_ref[rows, :] = grad_inflow * dt_w + skip_ref[...] * gy
        grad_inter_b = grad_inter.astype(bf16)
        gc_ref[rows, :] = (mm(enter_gy, old_b, NN) + mm(grad_inter_b, b_blk, NN)).astype(bf16)
        gb_ref[rows, :] = (mm(leave_in, later_b, NN) + mm(grad_inter_b, c_blk, TN)).astype(bf16)
        pass_col = jnp.sum(table_t * passing, 1, keepdims=True)
        grad_state[...] = pass_col * later + mm(enter_gy, c_blk, TN)
        return carry

    lax.fori_loop(0, blocks, one, 0)
    chunk = 256
    scale = HD ** (-0.5)
    gk_ref[...] = jnp.zeros_like(gk_ref)
    gv_ref[...] = jnp.zeros_like(gv_ref)
    for first in range(0, tokens, chunk):
        known = first + chunk
        rows = slice(first, known)
        q_pos = first + lax.broadcasted_iota(jnp.int32, (chunk, known), 0)
        k_pos = lax.broadcasted_iota(jnp.int32, (chunk, known), 1)
        allowed = (k_pos <= q_pos) & (segc_ref[rows, :] == segr_ref[:, :known])
        for head in range(q_heads):
            lanes = slice(head * HD, (head + 1) * HD)
            q_blk = q_ref[rows, lanes]
            grad_att = gm_ref[rows, lanes].astype(bf16)
            scores = mm(q_blk, k_ref[:known, :], NT) * scale
            scores = jnp.where(allowed, scores, masked_score)
            expo = jnp.exp(scores - jnp.max(scores, 1, keepdims=True))
            probs = expo / jnp.sum(expo, 1, keepdims=True)
            grad_probs = mm(grad_att, v_ref[:known, :], NT)
            gv_ref[:known, :] += mm(probs.astype(bf16), grad_att, TN)
            row_dot = jnp.sum(probs * grad_probs, 1, keepdims=True)
            grad_scores = (probs * (grad_probs - row_dot)).astype(bf16)
            gq_ref[rows, lanes] = mm(grad_scores, k_ref[:known, :], NN) * scale
            gk_ref[:known, :] += mm(grad_scores, q_blk, TN) * scale


def vmem_call(body, out_shape, scratch, name, flops, args):
    size = lambda a: a.size * a.dtype.itemsize
    moved = sum(size(a) for a in args) + sum(size(o) for o in out_shape)
    return pl.pallas_call(
        body,
        out_shape=tuple(out_shape),
        in_specs=[pl.BlockSpec(memory_space=pltpu.VMEM)] * len(args),
        out_specs=tuple([pl.BlockSpec(memory_space=pltpu.VMEM)] * len(out_shape)),
        scratch_shapes=scratch,
        name=name,
        compiler_params=pltpu.CompilerParams(vmem_limit_bytes=60 * 1024 * 1024),
        cost_estimate=pl.CostEstimate(flops=flops, bytes_accessed=moved, transcendentals=0),
    )(*args)


def ring_place():
    n = lax.axis_size("col")
    me = lax.axis_index("col")
    return n, me, lax.rem(me + 1, n), lax.rem(me + n - 1, n), lax.axis_index("row")


def meet(right, left, sibling):
    barrier = pltpu.get_barrier_semaphore()
    for place in ({"col": left}, {"col": right}, {"row": sibling}):
        pl.semaphore_signal(barrier, inc=1, device_id=place, device_id_type=pl.DeviceIdType.MESH)
    pl.semaphore_wait(barrier, 3)


def remote(source, target, send_sem, recv_sem, place):
    return pltpu.make_async_remote_copy(
        src_ref=source,
        dst_ref=target,
        send_sem=send_sem,
        recv_sem=recv_sem,
        device_id=place,
        device_id_type=pl.DeviceIdType.MESH,
    )


def gather_product_kernel(
    pieces, transpose, parts, shard_ref, w_ref, whole_ref, out_ref,
    x_all, w_mine, w_theirs, total, outgoing, incoming,
    ring_send, ring_recv, swap_send, swap_recv, load_sem, own_sem, save_sem, out_sem,
):
    n, me, right, left, row = ring_place()
    sibling = 1 - row
    count = shard_ref.shape[0]
    small = count // parts

    def weight_copies(held, which, base):
        copies, at = [], 0
        for index, (start, stride, size) in enumerate(pieces):
            first = pl.ds(pl.multiple_of(start + stride * which, 16), size)
            spot = pl.ds(at, size)
            if transpose:
                source, target = w_ref.at[first, :], held.at[spot, :]
            else:
                first = pl.ds(pl.multiple_of(start + stride * which, LANES), size)
                source, target = w_ref.at[:, first], held.at[:, spot]
            copies.append(pltpu.make_async_copy(source, target, load_sem.at[base + index]))
            at += size
        return copies

    loads = weight_copies(w_theirs, sibling, 0) + weight_copies(w_mine, row, len(pieces))
    own_rows = pl.ds(pl.multiple_of(me * count, count), count)
    own = pltpu.make_async_copy(shard_ref, x_all.at[own_rows, :], own_sem)
    own.start()
    for copy in loads:
        copy.start()
    meet(right, left, sibling)
    own.wait()

    def owner_of(step):
        return lax.rem(me - step + n, n)

    def ring(step, part):
        rows = pl.ds(pl.multiple_of(owner_of(step) * count + part * small, small), small)
        return remote(
            x_all.at[rows, :], x_all.at[rows, :], ring_send.at[step, part],
            ring_recv.at[step, part], {"col": right},
        )

    def rows_of(step):
        return pl.ds(pl.multiple_of(owner_of(step) * count, count), count)

    def swap(step):
        rows = rows_of(step)
        return remote(
            outgoing.at[rows, :], incoming.at[rows, :], swap_send.at[step], swap_recv.at[step],
            {"row": sibling},
        )

    def finish(step):
        rows = rows_of(step)
        swap(step).wait_recv()
        total[rows, :] = total[rows, :] + incoming[rows, :].astype(f32)
        pltpu.make_async_copy(total.at[rows, :], out_ref.at[rows, :], out_sem.at[step]).start()

    dims = NT if transpose else NN
    for part in range(parts):
        ring(0, part).start()
    for copy in loads:
        copy.wait()

    def one(step, carry):
        for part in range(parts):
            @pl.when(step > 0)
            def _():
                ring(step - 1, part).wait_recv()

            @pl.when((step > 0) & (step < n - 1))
            def _():
                ring(step, part).start()

        rows = rows_of(step)
        block = x_all[rows, :]
        outgoing[rows, :] = mm(block, w_theirs[...], dims).astype(outgoing.dtype)
        swap(step).start()
        total[rows, :] = mm(block, w_mine[...], dims)

        @pl.when(step > 0)
        def _():
            finish(step - 1)

        return carry

    lax.fori_loop(0, n, one, 0)
    save = pltpu.make_async_copy(x_all, whole_ref, save_sem)
    save.start()
    finish(n - 1)
    for step in range(n):
        rows = rows_of(step)
        pltpu.make_async_copy(total.at[rows, :], out_ref.at[rows, :], out_sem.at[step]).wait()
        swap(step).wait_send()
        if step < n - 1:
            for part in range(parts):
                ring(step, part).wait_send()
    save.wait()


def gather_product(shard, weight, pieces, transpose, ident):
    n = lax.axis_size("col")
    count, depth = shard.shape
    tokens = n * count
    width = sum(piece[2] for piece in pieces)
    parts = 2
    w_shape = (width, depth) if transpose else (depth, width)
    flops = 4 * tokens * depth * width
    return pl.pallas_call(
        functools.partial(gather_product_kernel, tuple(pieces), transpose, parts),
        out_shape=(
            jax.ShapeDtypeStruct((tokens, depth), bf16),
            jax.ShapeDtypeStruct((tokens, width), f32),
        ),
        in_specs=[pl.BlockSpec(memory_space=pl.ANY)] * 2,
        out_specs=(pl.BlockSpec(memory_space=pl.ANY), pl.BlockSpec(memory_space=pl.ANY)),
        scratch_shapes=[
            pltpu.VMEM((tokens, depth), bf16),
            pltpu.VMEM(w_shape, bf16),
            pltpu.VMEM(w_shape, bf16),
            pltpu.VMEM((tokens, width), f32),
            pltpu.VMEM((tokens, width), bf16),
            pltpu.VMEM((tokens, width), bf16),
            pltpu.SemaphoreType.DMA((n, parts)),
            pltpu.SemaphoreType.DMA((n, parts)),
            pltpu.SemaphoreType.DMA((n,)),
            pltpu.SemaphoreType.DMA((n,)),
            pltpu.SemaphoreType.DMA((2 * len(pieces),)),
            pltpu.SemaphoreType.DMA,
            pltpu.SemaphoreType.DMA,
            pltpu.SemaphoreType.DMA((n,)),
        ],
        name="gather_product_%d" % ident,
        compiler_params=pltpu.CompilerParams(
            collective_id=ident, has_side_effects=True, vmem_limit_bytes=40 * 1024 * 1024
        ),
        cost_estimate=pl.CostEstimate(
            flops=flops, bytes_accessed=6 * tokens * width + 120_000_000, transcendentals=0
        ),
    )(shard, weight)


def product_scatter_kernel(
    pieces, common, transpose, parts, *refs
):
    own_ref, refs = refs[0], refs[1:]
    both_ref = None
    if common:
        both_ref, refs = refs[0], refs[1:]
    (w_ref, whole_ref, out_ref, h_all, w_all, sums, outgoing, incoming, final,
     ring_send, ring_recv, swap_send, swap_recv, own_sem, both_sem, load_sem, save_sem, out_sem) = refs
    n, me, right, left, row = ring_place()
    sibling = 1 - row
    tokens = own_ref.shape[0]
    count = tokens // n
    small = count // parts

    def rows_of(step):
        chunk = lax.rem(me - 1 - step + 2 * n, n)
        return pl.ds(pl.multiple_of(chunk * count, count), count)

    def columns(which):
        spots, at = [], 0
        for start, stride, size in pieces:
            spots.append((pl.ds(at, size), pl.ds(pl.multiple_of(start + stride * which, LANES), size)))
            at += size
        return spots

    load = pltpu.make_async_copy(w_ref, w_all, load_sem)
    load.start()

    def own_copies(step):
        rows = rows_of(step)
        return [
            pltpu.make_async_copy(own_ref.at[rows, a], h_all.at[rows, b], own_sem.at[step, index])
            for index, (a, b) in enumerate(columns(row))
        ]

    def swaps(step):
        rows = rows_of(step)
        return [
            remote(own_ref.at[rows, a], h_all.at[rows, b], swap_send.at[step, index],
                   swap_recv.at[step, index], {"row": sibling})
            for index, (a, b) in enumerate(columns(row))
        ]

    def both_copy(step):
        rows = rows_of(step)
        return pltpu.make_async_copy(
            both_ref.at[rows, :], h_all.at[rows, pl.ds(common[0], common[1])], both_sem.at[step]
        )

    for step in range(n):
        for copy in own_copies(step):
            copy.start()
        if common:
            both_copy(step).start()
    meet(right, left, sibling)
    for step in range(n):
        for copy in swaps(step):
            copy.start()
    load.wait()
    dims = NT if transpose else NN

    def ring(step, part):
        rows = pl.ds(part * small, small)
        return remote(
            outgoing.at[step, rows, :], incoming.at[step, rows, :], ring_send.at[step, part],
            ring_recv.at[step, part], {"col": right},
        )

    def one(step, carry):
        rows = rows_of(step)
        for copy in own_copies(step):
            copy.wait()
        if common:
            both_copy(step).wait()
        for copy in swaps(step):
            copy.wait_recv()
        sums[...] = mm(h_all[rows, :], w_all[...], dims)
        for part in range(parts):
            some = pl.ds(part * small, small)

            @pl.when(step > 0)
            def _():
                ring(step - 1, part).wait_recv()
                sums[some, :] = sums[some, :] + incoming[step - 1, some, :].astype(f32)

            @pl.when(step < n - 1)
            def _():
                outgoing[step, some, :] = sums[some, :].astype(bf16)
                ring(step, part).start()

        return carry

    lax.fori_loop(0, n, one, 0)
    out = pltpu.make_async_copy(sums, out_ref, out_sem)
    out.start()
    save = pltpu.make_async_copy(h_all, whole_ref, save_sem)
    save.start()
    for step in range(n):
        for copy in swaps(step):
            copy.wait_send()
        if step < n - 1:
            for part in range(parts):
                ring(step, part).wait_send()
    out.wait()
    save.wait()


def product_scatter(own, weight, pieces, common, both, transpose, ident):
    n = lax.axis_size("col")
    tokens = own.shape[0]
    count = tokens // n
    depth, width = weight.shape[::-1] if transpose else weight.shape
    parts = 2
    operands = (own, both, weight) if common else (own, weight)
    return pl.pallas_call(
        functools.partial(product_scatter_kernel, tuple(pieces), common, transpose, parts),
        out_shape=(
            jax.ShapeDtypeStruct((tokens, depth), bf16),
            jax.ShapeDtypeStruct((count, width), f32),
        ),
        in_specs=[pl.BlockSpec(memory_space=pl.ANY)] * len(operands),
        out_specs=(pl.BlockSpec(memory_space=pl.ANY), pl.BlockSpec(memory_space=pl.ANY)),
        scratch_shapes=[
            pltpu.VMEM((tokens, depth), bf16),
            pltpu.VMEM(weight.shape, bf16),
            pltpu.VMEM((count, width), f32),
            pltpu.VMEM((n - 1, count, width), bf16),
            pltpu.VMEM((n - 1, count, width), bf16),
            pltpu.VMEM((8, LANES), f32),
            pltpu.SemaphoreType.DMA((n, parts)),
            pltpu.SemaphoreType.DMA((n, parts)),
            pltpu.SemaphoreType.DMA((n, len(pieces))),
            pltpu.SemaphoreType.DMA((n, len(pieces))),
            pltpu.SemaphoreType.DMA((n, len(pieces))),
            pltpu.SemaphoreType.DMA((n,)),
            pltpu.SemaphoreType.DMA,
            pltpu.SemaphoreType.DMA,
            pltpu.SemaphoreType.DMA,
        ],
        name="product_scatter_%d" % ident,
        compiler_params=pltpu.CompilerParams(
            collective_id=ident, has_side_effects=True, vmem_limit_bytes=40 * 1024 * 1024
        ),
        cost_estimate=pl.CostEstimate(
            flops=2 * tokens * depth * width, bytes_accessed=130_000_000, transcendentals=0
        ),
    )(*operands)


def shares_kernel(quarters, spans, held_ref, m_ref, v_ref, out_ref, zeros, taken, given, in_sem, out_sem, zero_sem):
    n = out_ref.shape[0]
    slot_rows = m_ref.shape[0] // 2
    zeros[...] = jnp.zeros_like(zeros)
    plan, at = [], 0
    for index, rows in enumerate(quarters):
        for source in (m_ref, v_ref):
            plan.append((index, rows, source, at))
            at += spans[index]
    for item, (index, rows, source, at) in enumerate(plan):
        blanks = [
            pltpu.make_async_copy(
                zeros.at[pl.ds(0, rows), :], out_ref.at[d, pl.ds(at, rows), :], zero_sem.at[item, d]
            )
            for d in range(n)
        ]

        @pl.when(held_ref[index] < 0)
        def _():
            for copy in blanks:
                copy.start()

    for item, (index, rows, source, at) in enumerate(plan):

        @pl.when(held_ref[index] >= 0)
        def _():
            base = held_ref[index] * slot_rows

            def fetch(d):
                first = pl.multiple_of(base + d * rows, 8)
                return pltpu.make_async_copy(
                    source.at[pl.ds(first, rows), :], taken.at[d % 2, pl.ds(0, rows), :],
                    in_sem.at[d % 2],
                )

            def store(d):
                return pltpu.make_async_copy(
                    given.at[d % 2, pl.ds(0, rows), :], out_ref.at[d, pl.ds(at, rows), :],
                    out_sem.at[d % 2],
                )

            fetch(0).start()
            for d in range(n):
                if d + 1 < n:
                    fetch(d + 1).start()
                fetch(d).wait()
                if d >= 2:
                    store(d - 2).wait()
                given[d % 2, pl.ds(0, rows), :] = taken[d % 2, pl.ds(0, rows), :].astype(bf16)
                store(d).start()
            for d in range(max(n - 2, 0), n):
                store(d).wait()

    for item, (index, rows, source, at) in enumerate(plan):
        blanks = [
            pltpu.make_async_copy(
                zeros.at[pl.ds(0, rows), :], out_ref.at[d, pl.ds(at, rows), :], zero_sem.at[item, d]
            )
            for d in range(n)
        ]

        @pl.when(held_ref[index] < 0)
        def _():
            for copy in blanks:
                copy.wait()


def moment_shares(held, moments, seconds, quarters, spans, n):
    largest = max(quarters)
    any_spec = pl.BlockSpec(memory_space=pl.ANY)
    total = 2 * sum(spans)
    return pl.pallas_call(
        functools.partial(shares_kernel, tuple(quarters), tuple(spans)),
        out_shape=jax.ShapeDtypeStruct((n, total, LANES), bf16),
        in_specs=[pl.BlockSpec(memory_space=pltpu.SMEM), any_spec, any_spec],
        out_specs=any_spec,
        scratch_shapes=[
            pltpu.VMEM((largest, LANES), bf16),
            pltpu.VMEM((2, largest, LANES), f32),
            pltpu.VMEM((2, largest, LANES), bf16),
            pltpu.SemaphoreType.DMA((2,)),
            pltpu.SemaphoreType.DMA((2,)),
            pltpu.SemaphoreType.DMA((2 * len(quarters), n)),
        ],
        name="moment_shares",
        cost_estimate=pl.CostEstimate(flops=0, bytes_accessed=45_000_000, transcendentals=0),
    )(held, moments, seconds)


def fresh_weight(grad, moment, second, weight):
    weight = weight.astype(f32)
    update = adam_step(grad.astype(f32), moment.astype(f32), second.astype(f32), weight)[2]
    return (weight + update).astype(bf16)


def share_step_kernel(g_ref, m_ref, v_ref, w_ref, out_ref):
    out_ref[...] = fresh_weight(g_ref[...], m_ref[...], v_ref[...], w_ref[...])


def share_step(grad, moment, second, weight):
    rows = grad.shape[0]
    block = min(rows, 1024)
    spec = pl.BlockSpec((block, LANES), lambda j: (j, 0))
    return pl.pallas_call(
        share_step_kernel,
        grid=(pl.cdiv(rows, block),),
        out_shape=jax.ShapeDtypeStruct((rows, LANES), bf16),
        in_specs=[spec] * 4,
        out_specs=spec,
        name="share_step",
        cost_estimate=pl.CostEstimate(
            flops=10 * grad.size, bytes_accessed=10 * grad.size, transcendentals=grad.size
        ),
    )(grad, moment, second, weight)


UNIT = 1648


def settle_kernel(held_ref, got_ref, m_ref, v_ref, w_ref, out_ref):
    @pl.when(held_ref[0] >= 0)
    def _():
        out_ref[...] = fresh_weight(
            got_ref[...], m_ref[...].astype(bf16), v_ref[...].astype(bf16), w_ref[...]
        )

    @pl.when(held_ref[0] < 0)
    def _():
        out_ref[...] = got_ref[...]


def settle(held, got, moments, seconds, weight):
    rows = got.shape[0]
    slot_blocks = moments.shape[0] // 2 // UNIT

    def state_at(j, held_ref):
        return (jnp.where(held_ref[0] >= 0, held_ref[0] * slot_blocks + j, 0), 0)

    def weight_at(j, held_ref):
        return (jnp.where(held_ref[0] >= 0, j, 0), 0)

    plain = pl.BlockSpec((UNIT, LANES), lambda j, held_ref: (j, 0))
    return pl.pallas_call(
        settle_kernel,
        grid_spec=pltpu.PrefetchScalarGridSpec(
            num_scalar_prefetch=1,
            grid=(pl.cdiv(rows, UNIT),),
            in_specs=[
                plain,
                pl.BlockSpec((UNIT, LANES), state_at),
                pl.BlockSpec((UNIT, LANES), state_at),
                pl.BlockSpec((UNIT, LANES), weight_at),
            ],
            out_specs=plain,
        ),
        out_shape=jax.ShapeDtypeStruct((rows, LANES), bf16),
        name="settle",
        cost_estimate=pl.CostEstimate(
            flops=10 * got.size, bytes_accessed=12 * got.size, transcendentals=got.size
        ),
    )(held, got, moments, seconds, weight)


def owner_kernel(sizes, which_ref, block_ref, m_ref, v_ref, *refs):
    g_refs, w_refs = refs[:MATS], refs[MATS : 2 * MATS]
    grad_ref, m_out, v_out, u_out = refs[2 * MATS :]
    step = pl.program_id(0)
    which = which_ref[step]
    rows = block_ref[step] * UNIT + lax.broadcasted_iota(jnp.int32, (UNIT, LANES), 0)

    @pl.when(which < 0)
    def _():
        for out in (grad_ref, m_out, v_out, u_out):
            out[...] = jnp.zeros_like(out)

    for index in range(MATS):

        @pl.when(which == index)
        def _():
            inside = rows < sizes[index]
            grad = jnp.where(inside, g_refs[index][...].astype(f32), 0.0)
            weight = jnp.where(inside, w_refs[index][...].astype(f32), 0.0)
            grad_ref[...] = grad
            m_out[...], v_out[...], u_out[...] = adam_step(grad, m_ref[...], v_ref[...], weight)


def owner_outputs(which, block, moments, seconds, grads, weights):
    rows = moments.shape[0]
    sizes = tuple(g.shape[0] for g in grads)

    def chosen(index):
        last = pl.cdiv(sizes[index], UNIT) - 1

        def at(j, which_ref, block_ref):
            return (jnp.where(which_ref[j] == index, jnp.minimum(block_ref[j], last), 0), 0)

        return pl.BlockSpec((UNIT, LANES), at)

    plain = pl.BlockSpec((UNIT, LANES), lambda j, which_ref, block_ref: (j, 0))
    picks = [chosen(index) for index in range(MATS)]
    return pl.pallas_call(
        functools.partial(owner_kernel, sizes),
        grid_spec=pltpu.PrefetchScalarGridSpec(
            num_scalar_prefetch=2,
            grid=(rows // UNIT,),
            in_specs=[plain, plain] + picks + picks,
            out_specs=[plain] * 4,
        ),
        out_shape=[jax.ShapeDtypeStruct((rows, LANES), f32)] * 4,
        name="owner_outputs",
        cost_estimate=pl.CostEstimate(
            flops=12 * rows * LANES, bytes_accessed=26 * rows * LANES, transcendentals=rows * LANES
        ),
    )(which, block, moments, seconds, *grads, *weights)


def row_total(values):
    return lax.psum(values, "row")


def conv_shift(values, segments, lag):
    if lag == 0:
        return values
    tokens = values.shape[0]
    pad = jnp.zeros((abs(lag), values.shape[1]), values.dtype)
    foreign = jnp.full((abs(lag),), -1, jnp.int32)
    if lag > 0:
        moved = jnp.concatenate([pad, values[: tokens - lag]], 0)
        other = jnp.concatenate([foreign, segments[: tokens - lag]], 0)
    else:
        moved = jnp.concatenate([values[-lag:], pad], 0)
        other = jnp.concatenate([segments[-lag:], foreign], 0)
    return jnp.where((other == segments)[:, None], moved, 0.0)


def norm_back(grad_act, normed, scale_rows, gain):
    weighted = grad_act * gain
    inner_sum = row_total(jnp.sum(weighted * normed, 1))
    grad_in = scale_rows[:, None] * (weighted - normed * (inner_sum / D)[:, None])
    return (grad_in, jnp.sum(grad_act * normed, 0))


def shards(
    x_in,
    cotangent,
    segment_ids,
    owner,
    w_mix_in,
    w_mix_out,
    w_gate_up,
    w_down,
    mat_m,
    mat_v,
    small_params,
    small_m,
    small_v,
):
    n_row = lax.axis_size("row")
    n_col = lax.axis_size("col")
    n_dp = lax.axis_size("dp")
    row_index = lax.axis_index("row")
    col_index = lax.axis_index("col")
    dp_index = lax.axis_index("dp")
    tokens = SEQ
    width_row = x_in.shape[1]
    q_width = QH * HD // n_col
    sub = STATE // n_col
    shared_width = 4 * sub
    ssm_width = SH * SP // n_col
    head_count = SH // n_col
    ff_width = FF // n_col
    mix_width = q_width + ssm_width
    conv_width = SH * SP + 2 * STATE
    col_z = q_width + shared_width
    col_x = col_z + ssm_width
    col_dt = col_x + ssm_width
    q_own = q_width // n_row
    ssm_own = ssm_width // n_row
    heads = head_count // n_row
    q_heads = q_own // HD
    ff_own = ff_width // n_row
    at_kv = q_own
    at_z = at_kv + shared_width
    at_x = at_z + ssm_own
    at_dt = at_x + ssm_own
    segs = segment_ids[0]

    off_alog = 2 * D
    off_dtb = 2 * D + SH
    off_skip = 2 * D + 2 * SH
    off_kern = 2 * D + 3 * SH
    off_cbias = off_kern + CONV * conv_width
    first_head = col_index * head_count + row_index * heads
    gain_one = lax.dynamic_slice_in_dim(small_params, row_index * width_row, width_row)
    gain_two = lax.dynamic_slice_in_dim(small_params, D + row_index * width_row, width_row)

    def own_heads(offset):
        return lax.dynamic_slice_in_dim(small_params, offset + first_head, heads)

    a_log_own, dt_bias_own, skip_own = own_heads(off_alog), own_heads(off_dtb), own_heads(off_skip)
    conv_table = small_params[off_kern:].reshape(CONV + 1, conv_width)

    def own_channels(table):
        return jnp.concatenate(
            [
                lax.dynamic_slice_in_dim(table, SH * SP + col_index * sub, sub, 1),
                lax.dynamic_slice_in_dim(table, SH * SP + STATE + col_index * sub, sub, 1),
                lax.dynamic_slice_in_dim(table, first_head * SP, ssm_own, 1),
            ],
            1,
        )

    conv_own = own_channels(conv_table)
    kern_own, bias_own = conv_own[:CONV], conv_own[CONV]
    rate = -jnp.exp(a_log_own)

    def pad_heads(values):
        return jnp.pad(values, [(0, 0)] * (values.ndim - 1) + [(0, 8 - heads)])

    w_in_t = w_mix_in.T
    dt_rows = w_in_t[col_dt:].reshape(n_row, heads, width_row)
    dt_rows = jnp.pad(dt_rows, ((0, 0), (0, LANES - heads), (0, 0)))

    w_in_full = jnp.concatenate([w_in_t[:col_dt], dt_rows.reshape(n_row * LANES, width_row)], 0)

    xf = x_in.astype(f32)
    scale_one = lax.rsqrt(row_total(jnp.sum(xf * xf, 1)) / D + norm_eps)
    normed_one = xf * scale_one[:, None]
    act_one = (normed_one * gain_one).astype(bf16)
    in_pieces = [
        (0, q_own, q_own),
        (q_width, 0, shared_width),
        (col_z, ssm_own, ssm_own),
        (col_x, ssm_own, ssm_own),
        (col_dt, LANES, LANES),
    ]
    gu_pieces = [(0, ff_own, ff_own), (ff_width, ff_own, ff_own)]
    mix_pieces = [(0, q_own, q_own), (q_width, ssm_own, ssm_own)]
    down_pieces = [(0, ff_own, ff_own)]
    act_one_g, proj = gather_product(act_one, w_in_full, in_pieces, True, 0)

    queries = proj[:, :at_kv].astype(bf16)
    kv_own = proj[:, at_kv : at_kv + 2 * sub]
    z_gate = proj[:, at_z:at_x]
    dt_raw = proj[:, at_dt : at_dt + heads]
    conv_in = jnp.concatenate([proj[:, at_kv + 2 * sub : at_z], proj[:, at_x:at_dt]], 1)
    conv_out = bias_own
    for lag in range(CONV):
        conv_out = conv_out + kern_own[lag] * conv_shift(conv_in, segs, lag)
    bc_pre, x_pre = conv_out[:, : 2 * sub], conv_out[:, 2 * sub :]
    x_sig = silu_value(x_pre).astype(bf16)
    shared = jnp.concatenate([kv_own, silu_value(bc_pre)], 1).astype(bf16)
    half = tokens // n_row
    shared_half = lax.dynamic_slice_in_dim(shared, row_index * half, half)
    features = lax.all_gather(shared_half, ("row", "col"), axis=0)
    features = features.reshape(n_row, n_col, half, 4, sub).transpose(3, 0, 2, 1, 4)
    features = features.reshape(4, tokens, STATE)
    q_local = QH // n_col
    kv_head = col_index * q_local // (QH // KVH)
    key_head = lax.dynamic_slice_in_dim(features[0], kv_head * HD, HD, 1)
    val_head = lax.dynamic_slice_in_dim(features[1], kv_head * HD, HD, 1)
    b_mat, c_mat = features[2], features[3]

    dt = jax.nn.softplus(dt_raw + dt_bias_own)
    dt_pad = pad_heads(dt)
    a_pad = pad_heads(dt * rate)
    seg_blocks = segs.reshape(tokens // SPAN, SPAN)
    before = jnp.concatenate([jnp.full((1,), -1, jnp.int32), seg_blocks[:-1, -1]])
    same_prev = (seg_blocks == before[:, None]).reshape(tokens)
    same_last = (seg_blocks == seg_blocks[:, -1:]).reshape(tokens)
    meta = jnp.stack([same_prev, same_last], 1).astype(f32)
    seg_col, seg_row = segs[:, None], segs[None, :]
    skip_wide = jnp.repeat(skip_own, SP)[None, :]
    common = (dt_pad, a_pad, a_pad.T, meta, seg_col, seg_row, skip_wide)
    n_blocks = tokens // SPAN
    mix_own, y_ssm, states = vmem_call(
        functools.partial(mixer_forward_kernel, heads, q_heads),
        [
            jax.ShapeDtypeStruct((tokens, q_own + ssm_own), bf16),
            jax.ShapeDtypeStruct((tokens, ssm_own), f32),
            jax.ShapeDtypeStruct((n_blocks, ssm_own, STATE), f32),
        ],
        [pltpu.VMEM((ssm_own, STATE), f32)],
        "mixer_forward",
        1_000_000_000,
        (queries, key_head, val_head, x_sig, z_gate, b_mat, c_mat) + common,
    )
    mix_g, mix_sum = product_scatter(mix_own, w_mix_out, mix_pieces, None, None, False, 1)
    hidden_one = xf + mix_sum
    scale_two = lax.rsqrt(row_total(jnp.sum(hidden_one * hidden_one, 1)) / D + norm_eps)
    normed_two = hidden_one * scale_two[:, None]
    act_two = (normed_two * gain_two).astype(bf16)
    act_two_g, gate_up = gather_product(act_two, w_gate_up, gu_pieces, False, 2)
    gate, upper = gate_up[:, :ff_own], gate_up[:, ff_own:]
    inner = (silu_value(gate) * upper).astype(bf16)
    inner_g, down_sum = product_scatter(inner, w_down, down_pieces, None, None, False, 3)
    y_out = (hidden_one + down_sum).astype(bf16)

    grad_out_g, grad_inner = gather_product(cotangent, w_down, down_pieces, True, 4)
    grad_down_w = mm(inner_g, grad_out_g, TN).astype(bf16)
    grad_gu = jnp.concatenate(
        [grad_inner * upper * silu_slope(gate), grad_inner * silu_value(gate)], 1
    ).astype(bf16)
    grad_gu_g, grad_act_two = product_scatter(grad_gu, w_gate_up, gu_pieces, None, None, True, 5)
    grad_gu_w = mm(act_two_g, grad_gu_g, TN).astype(bf16)
    grad_norm_two, gain_two_part = norm_back(grad_act_two, normed_two, scale_two, gain_two)
    grad_hidden = cotangent.astype(f32) + grad_norm_two
    grad_hidden_g, grad_mix = gather_product(
        grad_hidden.astype(bf16), w_mix_out, mix_pieces, True, 6
    )
    grad_mix_w = mm(mix_g, grad_hidden_g, TN).astype(bf16)

    shape = lambda cols, kind: jax.ShapeDtypeStruct((tokens, cols), kind)
    grad_q, grad_k, grad_v, grad_z, grad_x, grad_dt, grad_b, grad_c, small_sums, grad_skip = vmem_call(
        functools.partial(mixer_backward_kernel, heads, q_heads),
        [
            shape(q_own, f32), shape(HD, f32), shape(HD, f32), shape(ssm_own, f32),
            shape(ssm_own, f32), shape(8, f32), shape(STATE, bf16), shape(STATE, bf16),
            jax.ShapeDtypeStruct((8, 8), f32), jax.ShapeDtypeStruct((1, ssm_own), f32),
        ],
        [pltpu.VMEM((ssm_own, STATE), f32)],
        "mixer_backward",
        3_000_000_000,
        (grad_mix, queries, key_head, val_head, x_sig, z_gate, y_ssm, b_mat, c_mat)
        + common
        + (pad_heads(rate)[None, :], states),
    )
    zero_kv = jnp.zeros((tokens, KVH * HD), bf16)
    keys_full = lax.dynamic_update_slice(zero_kv, grad_k.astype(bf16), (0, kv_head * HD))
    vals_full = lax.dynamic_update_slice(zero_kv, grad_v.astype(bf16), (0, kv_head * HD))
    term = jnp.stack([keys_full, vals_full, grad_b, grad_c], 1)
    term = term.reshape(n_row, half, 4, n_col, sub).transpose(0, 3, 1, 2, 4)
    term = term.reshape(n_row * n_col, half, shared_width)
    shared_sum = lax.psum_scatter(term, ("row", "col"), scatter_dimension=0, tiled=False)
    grad_shared = lax.all_gather(shared_sum, "row", axis=0, tiled=True).astype(f32)
    grad_conv = jnp.concatenate(
        [grad_shared[:, 2 * sub :] * silu_slope(bc_pre), grad_x * silu_slope(x_pre)], 1
    ).astype(bf16).astype(f32)
    bias_grad = jnp.sum(grad_conv, 0)
    grad_conv_raw = kern_own[0] * grad_conv
    kern_grad = [jnp.sum(grad_conv * conv_in, 0)]
    for lag in range(1, CONV):
        grad_conv_raw = grad_conv_raw + kern_own[lag] * conv_shift(grad_conv, segs, -lag)
        kern_grad.append(jnp.sum(grad_conv * conv_shift(conv_in, segs, lag), 0))
    kern_grad = jnp.stack(kern_grad)
    raw_own = jnp.concatenate(
        [grad_q, grad_z, grad_conv_raw[:, 2 * sub :], jnp.pad(grad_dt, ((0, 0), (0, LANES - 8)))], 1
    ).astype(bf16)
    raw_kvbc = jnp.concatenate([grad_shared[:, : 2 * sub], grad_conv_raw[:, : 2 * sub]], 1).astype(bf16)
    raw_pieces = [piece for index, piece in enumerate(in_pieces) if index != 1]
    raw_g, grad_act_one = product_scatter(
        raw_own, w_in_full, raw_pieces, (q_width, shared_width), raw_kvbc, False, 7
    )
    in_w = mm(act_one_g, raw_g, TN).astype(bf16)
    grad_in_w = jnp.concatenate(
        [in_w[:, :col_dt]]
        + [in_w[:, col_dt + r * LANES : col_dt + r * LANES + heads] for r in range(n_row)],
        1,
    )
    grad_norm_one, gain_one_part = norm_back(grad_act_one, normed_one, scale_one, gain_one)
    x_grad = (grad_hidden + grad_norm_one).astype(bf16)

    small_own = jnp.concatenate(
        [
            gain_one_part,
            gain_two_part,
            small_sums[0, :heads] * rate,
            small_sums[1, :heads],
            jnp.sum(grad_skip.reshape(heads, SP), 1),
            kern_grad.reshape(-1),
            bias_grad,
        ]
    )
    small_len = small_own.shape[0]
    small_rows = -(-small_len // (8 * LANES)) * 8
    small_own = jnp.pad(small_own, (0, small_rows * LANES - small_len)).reshape(small_rows, LANES)
    everyone = lax.all_gather(small_own, ("dp", "row", "col"), axis=0, tiled=True)
    everyone = everyone.reshape(n_dp, n_row, n_col, small_rows * LANES)
    total = jnp.sum(everyone, 0)[..., :small_len]
    pieces = jnp.split(
        total,
        [
            width_row, 2 * width_row, 2 * width_row + heads, 2 * width_row + 2 * heads,
            2 * width_row + 3 * heads,
        ],
        axis=2,
    )

    def by_head(values):
        return values.transpose(1, 0, 2).reshape(-1)

    conv_sum = pieces[5].reshape(n_row, n_col, CONV + 1, 2 * sub + ssm_own)
    x_sum = conv_sum[..., 2 * sub :].transpose(2, 1, 0, 3).reshape(CONV + 1, SH * SP)
    b_sum = conv_sum[0, ..., :sub].transpose(1, 0, 2).reshape(CONV + 1, STATE)
    c_sum = conv_sum[0, ..., sub : 2 * sub].transpose(1, 0, 2).reshape(CONV + 1, STATE)
    small_grad = jnp.concatenate(
        [
            jnp.sum(pieces[0], 1).reshape(-1),
            jnp.sum(pieces[1], 1).reshape(-1),
            by_head(pieces[2]),
            by_head(pieces[3]),
            by_head(pieces[4]),
            jnp.concatenate([x_sum, b_sum, c_sum], 1).reshape(-1),
        ]
    )
    small_moment, small_second, small_update = adam_step(small_grad, small_m, small_v, small_params)

    weights_local = (w_mix_in, w_mix_out, w_gate_up, w_down)
    grads_local = (grad_in_w, grad_mix_w, grad_gu_w, grad_down_w)
    group_size = n_dp // OWNERS
    piece_len = mat_m.shape[-1]
    my_group = dp_index // group_size
    my_piece = dp_index % group_size
    sizes = [w.size for w in weights_local]
    slot_len = max(sizes)
    moments = mat_m.reshape(piece_len // LANES, LANES)
    seconds = mat_v.reshape(piece_len // LANES, LANES)
    slot_rows = slot_len // LANES
    rows_of = [size // LANES for size in sizes]
    quarters = [rows // n_dp for rows in rows_of]
    spans = [-(-rows // 32) * 32 for rows in quarters]
    ranks = []
    for index in range(MATS):
        earlier = jnp.int32(0)
        for other in range(index):
            earlier = earlier + (owner[other] == owner[index]).astype(jnp.int32)
        ranks.append(earlier)
    held = jnp.stack([jnp.where(owner[i] == my_group, ranks[i], -1) for i in range(MATS)])

    def flat(matrix):
        return matrix.reshape(-1, LANES)

    def own_share(matrix):
        count = matrix.shape[0] // n_dp
        return flat(lax.dynamic_slice_in_dim(matrix, dp_index * count, count))

    def share_sum(values):
        count, width = values.shape[1:]
        values = values.reshape(n_dp * count, width)
        return lax.psum_scatter(values, "dp", scatter_dimension=0, tiled=True)

    def in_shares(values, index):
        values = values.reshape(n_dp, quarters[index], LANES)
        return jnp.pad(values, ((0, 0), (0, spans[index] - quarters[index]), (0, 0)))

    if group_size == 1:
        shares = moment_shares(held, moments, seconds, quarters, spans, n_dp)
    else:
        parts = []
        for index in range(MATS):
            at = ranks[index] * slot_rows - my_piece * moments.shape[0]
            entry = jnp.arange(rows_of[index]) + at
            inside = (held[index] >= 0) & (entry >= 0) & (entry < moments.shape[0])
            for buffer in (moments, seconds):
                wide = jnp.pad(buffer, ((slot_rows, slot_rows), (0, 0)))
                first = jnp.clip(at + slot_rows, 0, moments.shape[0] + slot_rows)
                cut = lax.dynamic_slice_in_dim(wide, first, rows_of[index])
                cut = jnp.where(inside[:, None], cut, 0.0).astype(bf16)
                parts.append(in_shares(cut, index))
        shares = jnp.concatenate(parts, 1)
    shares = share_sum(shares)
    moment_share, second_share, at = [], [], 0
    for rows, span in zip(quarters, spans):
        moment_share.append(shares[at : at + rows])
        second_share.append(shares[at + span : at + span + rows])
        at += 2 * span

    flat_w = [flat(w) for w in weights_local]
    flat_g, new_weights = [None] * MATS, [None] * MATS
    for group in ((3, 2), (1, 0)):
        cut = jnp.concatenate([in_shares(flat(grads_local[i]), i) for i in group], 1)
        cut = share_sum(cut)
        grad_share, fresh_share, at = {}, {}, 0
        for i in group:
            grad_share[i] = cut[at : at + quarters[i]]
            fresh_share[i] = share_step(
                grad_share[i], moment_share[i], second_share[i], own_share(weights_local[i])
            )
            at += spans[i]
        if group_size == 1:
            sent = jnp.concatenate(
                [
                    jnp.where(
                        (owner[i] == jnp.arange(n_dp))[:, None, None],
                        grad_share[i][None],
                        fresh_share[i][None],
                    )
                    for i in group
                ],
                1,
            )
            got = lax.all_to_all(sent, "dp", 0, 0)
            at = 0
            for i in group:
                flat_g[i] = got[:, at : at + quarters[i]].reshape(rows_of[i], LANES)
                fresh = settle(held[i : i + 1], flat_g[i], moments, seconds, flat_w[i])
                new_weights[i] = fresh.reshape(weights_local[i].shape)
                at += quarters[i]
        else:
            both = jnp.concatenate([grad_share[i] for i in group] + [fresh_share[i] for i in group], 0)
            got = lax.all_gather(both, "dp", axis=0)
            at, half_rows = 0, both.shape[0] // 2
            for i in group:
                flat_g[i] = got[:, at : at + quarters[i]].reshape(rows_of[i], LANES)
                fresh = got[:, half_rows + at : half_rows + at + quarters[i]]
                new_weights[i] = fresh.reshape(weights_local[i].shape)
                at += quarters[i]

    first_row = my_piece * moments.shape[0] + jnp.arange(moments.shape[0] // UNIT) * UNIT
    which = jnp.full(first_row.shape, -1, jnp.int32)
    for index in range(MATS):
        which = jnp.where(held[index] == first_row // slot_rows, index, which)
    block = (first_row % slot_rows // UNIT).astype(jnp.int32)
    grad_piece, moment_new, second_new, update = owner_outputs(
        which.astype(jnp.int32), block, moments, seconds, flat_g, flat_w
    )
    out_shape = (1, 1, 1, piece_len)
    return (
        y_out,
        x_grad,
        grad_piece.reshape(out_shape),
        moment_new.reshape(out_shape),
        second_new.reshape(out_shape),
        update.reshape(out_shape),
        new_weights[0],
        new_weights[1],
        new_weights[2],
        new_weights[3],
        small_grad,
        small_moment,
        small_second,
        small_update,
    )


def solution(mesh):
    placed = (
        P(("dp", "col"), "row"),
        P(("dp", "col"), "row"),
        P("dp", None),
        P(),
        P("row", "col"),
        P("col", "row"),
        P("row", "col"),
        P("col", "row"),
        P("row", "col", "dp", None),
        P("row", "col", "dp", None),
        P(),
        P(),
        P(),
    )
    return jax.shard_map(
        shards,
        mesh=mesh,
        in_specs=placed,
        out_specs=(
            P(("dp", "col"), "row"),
            P(("dp", "col"), "row"),
            P("row", "col", "dp", None),
            P("row", "col", "dp", None),
            P("row", "col", "dp", None),
            P("row", "col", "dp", None),
            P("row", "col"),
            P("col", "row"),
            P("row", "col"),
            P("col", "row"),
            P(),
            P(),
            P(),
            P(),
        ),
        check_vma=False,
    )
```

time: 1990 us -> 1240 us (0.62)
  waiting for transfers between devices: 1020 us -> 242 us
  Pallas kernels: 0 us -> 538 us
  other arithmetic: 336 us -> 77.4 us
  matrix products: 207 us -> 22.9 us
  local copies, waits for them, and re-layouts: 353 us -> 226 us
  blocking collectives: 22.1 us -> 91.9 us
    pallas_call x0 -> x20, Pallas kernels: none -> 538 us  [the longest x4 191 us: product_scatter(): pl.pallas_call(functools.partial(product_scatter_kernel, tuple(pieces), c...]
    all_gather x10 -> x1, waiting for transfers between devices: 525 us -> 0.01 us  [shards(): features = lax.all_gather(shared_half, ('row', 'col'), axis=0)]
    psum x2 -> x0, waiting for transfers between devices: 282 us -> none  [the longest x1 178 us: shards(): lax.psum(grad_in_w.astype(jnp.bfloat16), 'dp').astype(jnp.float32)]
    dot_general x71 -> x4, matrix products: 207 us -> 22.9 us  [mm(): lax.dot_general(left, right, (dims, ((), ())), preferred_element_type=f32...]
    dynamic_update_slice x68 -> x2, local copies, waits for them, and re-layouts: 126 us -> 0.05 us  [the longest x1 0.02 us: shards(): lax.dynamic_update_slice(zero_kv, grad_v.astype(bf16), (0, kv_head * HD))]
    all_gather x4 -> x2, blocking collectives: 9.47 us -> 81.7 us  [the longest x1 79.2 us: shards(): lax.all_gather(small_own, ('dp', 'row', 'col'), axis=0, tiled=True)]
    convert_element_type x25 -> x7, other arithmetic: 73.5 us -> 7.52 us  [the longest x1 3.07 us: shards(): x_grad = (grad_hidden + grad_norm_one).astype(bf16)]
    select_n x9 -> x6, other arithmetic: 53.1 us -> 3.06 us  [the longest x4 1.92 us: shards(): jnp.where((owner[i] == jnp.arange(n_dp))[:, None, None], grad_share[i][No...]
  transfers between devices with their start and end apart: 23 -> 7, of which waited for: 18 -> 2; matrix products, arithmetic and copies ran while one was open for 28% -> 17% of each run, Pallas kernels for 0% -> 17%
where the time goes in v1:
time: 1240 us; the launch traced here: 1230 us
  Pallas kernels  538 us (43%)
  waiting for transfers between devices  242 us (20%)
  local copies, waits for them, and re-layouts  226 us (18%)
  blocking collectives  91.9 us (7%)
  other arithmetic  77.4 us (6%)
  between operations  25.1 us (2%)
  matrix products  22.9 us (2%)
    reduce_scatter x3, waiting for transfers between devices, share_sum(): return lax.psum_scatter(values, 'dp', scatter_dimension=0, tiled=True)  242 us
    pallas_call x4, Pallas kernels, product_scatter(): pl.pallas_call(functools.partial(product_scatter_kernel, tuple(pieces), c...  191 us
    pallas_call x4, Pallas kernels, gather_product(): pl.pallas_call(functools.partial(gather_product_kernel, tuple(pieces), tr...  174 us
    all_gather x1, blocking collectives, shards(): lax.all_gather(small_own, ('dp', 'row', 'col'), axis=0, tiled=True)  79.2 us
    pallas_call x1, Pallas kernels, owner_outputs(): pl.pallas_call(functools.partial(owner_kernel, sizes), grid_spec=pltpu.Pr...  47.9 us
    pallas_call x2, Pallas kernels, vmem_call(): pl.pallas_call(body, out_shape=tuple(out_shape), in_specs=[pl.BlockSpec(m...  46.3 us
    unnamed x158, local copies, waits for them, and re-layouts  39.8 us
    reshape x8, local copies, waits for them, and re-layouts, flat(): return matrix.reshape(-1, LANES)  39.1 us
  transfers between devices with their start and end apart: 7, of which 2 were waited for; matrix products, arithmetic and copies ran while one was open for 17% of the time, Pallas kernels for 17%

profile of v1, /device:TPU:0, one launch (start us, length us, event | category | flops | bytes accessed | tf_op | source)
XLA Modules:
  0.0 1234.3 jit_solution(9637876710128114394)
XLA Ops:
  18.7 43.5 %gather_product_0.1 = (bf16[1024,1024]{1,0:T(8,128)(2,1)S(1)}, f32[1024,1280]{1,0:T(8,128)S(1)}) custom-call(bf16[256,1024]{1,0:T(8,128)(2,1)S(1)} %fusion.20.shard_ref, bf16[2304,1024]{1,0:T(8,128)(2,1)S(1)} %pad_maximum_fusion.3.w_ref.refs_2_), custom_call_target="tpu_custom_call" | custom-call | flops 5368709120 | bytes 127864320 | tf_op jit(solution)/shard_map/gather_product_0/pallas_call | solution.py:412
  81.0 5.9 copy.163
  96.5 48.2 %gather_product_4.1 = (bf16[1024,1024]{1,0:T(8,128)(2,1)S(1)}, f32[1024,512]{1,0:T(8,128)S(1)}) custom-call(bf16[256,1024]{1,0:T(8,128)(2,1)S(1)} %copy-done.9, bf16[1024,1024]{1,0:T(8,128)(2,1)S(1)} %copy-done.4), custom_call_target="tpu_custom_call" | custom-call | flops 2147483648 | bytes 123145728 | tf_op jit(solution)/shard_map/gather_product_4/pallas_call | solution.py:412
  167.6 16.5 %mixer_forward.1 = (bf16[1024,512]{1,0:T(8,128)(2,1)}, f32[1024,384]{1,0:T(8,128)}, f32[8,384,256]{2,1,0:T(8,128)}) custom-call(bf16[1024,128]{1,0:T(8,128)(2,1)} %get-tuple-element.181.q_ref, bf16[1024,128]{1,0:T(8,128)(2,1)} %get-tuple-element.225.k_ref, bf16[1024,128]{1,0:T(8,128)(2,1)} %get-tuple-element.224.v_ref, ...), custom_call_target="tpu_custom_call" | custom-call | flops 1000000000 | bytes 10077696 | tf_op jit(solution)/shard_map/mixer_forward/pallas_call | solution.py:267
  185.3 41.7 %product_scatter_1.1 = (bf16[1024,1024]{1,0:T(8,128)(2,1)S(1)}, f32[256,1024]{1,0:T(8,128)S(1)}) custom-call(bf16[1024,512]{1,0:T(8,128)(2,1)S(1)} %copy-done.13, bf16[1024,1024]{1,0:T(8,128)(2,1)S(1)} %copy-done.3), custom_call_target="tpu_custom_call" | custom-call | flops 2147483648 | bytes 130000000 | tf_op jit(solution)/shard_map/product_scatter_1/pallas_call | solution.py:561
  233.2 41.5 %gather_product_2.1 = (bf16[1024,1024]{1,0:T(8,128)(2,1)S(1)}, f32[1024,1024]{1,0:T(8,128)S(1)}) custom-call(bf16[256,1024]{1,0:T(8,128)(2,1)S(1)} %multiply_convert_fusion.5.shard_ref, bf16[1024,2048]{1,0:T(8,128)(2,1)S(1)} %copy-done.1), custom_call_target="tpu_custom_call" | custom-call | flops 4294967296 | bytes 126291456 | tf_op jit(solution)/shard_map/gather_product_2/pallas_call | solution.py:412
  277.5 42.9 %product_scatter_5.1 = (bf16[1024,2048]{1,0:T(8,128)(2,1)S(1)}, f32[256,1024]{1,0:T(8,128)S(1)}) custom-call(bf16[1024,1024]{1,0:T(8,128)(2,1)S(1)} %pad_maximum_fusion.6.refs_0_, bf16[1024,2048]{1,0:T(8,128)(2,1)S(1)} %copy-done.1), custom_call_target="tpu_custom_call" | custom-call | flops 4294967296 | bytes 130000000 | tf_op jit(solution)/shard_map/product_scatter_5/pallas_call | solution.py:561
  326.9 40.8 %gather_product_6.1 = (bf16[1024,1024]{1,0:T(8,128)(2,1)S(1)}, f32[1024,512]{1,0:T(8,128)S(1)}) custom-call(bf16[256,1024]{1,0:T(8,128)(2,1)S(1)} %fusion.31.shard_ref, bf16[1024,1024]{1,0:T(8,128)(2,1)S(1)} %copy-done.3), custom_call_target="tpu_custom_call" | custom-call | flops 2147483648 | bytes 123145728 | tf_op jit(solution)/shard_map/gather_product_6/pallas_call | solution.py:412
  370.4 29.7 %mixer_backward.1 = (f32[1024,128]{1,0:T(8,128)}, f32[1024,128]{1,0:T(8,128)}, f32[1024,128]{1,0:T(8,128)}, f32[1024,384]{1,0:T(8,128)}, f32[1024,384]{1,0:T(8,1...) custom-call(f32[1024,512]{1,0:T(8,128)} %copy-done.6, ...), custom_call_target="tpu_custom_call" | custom-call | flops 3000000000 | bytes 16928032 | tf_op jit(solution)/shard_map/mixer_backward/pallas_call | solution.py:267
  414.9 8.5 convolution_convert_fusion.1
  423.3 7.5 reshape_reshape.15
  432.1 63.0 %product_scatter_3.1 = (bf16[1024,1024]{1,0:T(8,128)(2,1)S(1)}, f32[256,1024]{1,0:T(8,128)S(1)}) custom-call(bf16[1024,512]{1,0:T(8,128)(2,1)S(1)} %copy-done.11, bf16[1024,1024]{1,0:T(8,128)(2,1)S(1)} %copy-done.5), custom_call_target="tpu_custom_call" | custom-call | flops 2147483648 | bytes 130000000 | tf_op jit(solution)/shard_map/product_scatter_3/pallas_call | solution.py:561
  519.6 25.4 %moment_shares.1 = bf16[4,24640,128]{2,1,0:T(8,128)(2,1)} custom-call(s32[4]{0:T(128)} %pad_add_fusion.2.held_ref, f32[32960,128]{1,0:T(8,128)} %bitcast.113, f32[32960,128]{1,0:T(8,128)} %bitcast.119), custom_call_target="tpu_custom_call" | custom-call | bytes 45000000 | tf_op jit(solution)/shard_map/moment_shares/pallas_call | solution.py:667
  570.7 43.6 %product_scatter_7.1 = (bf16[1024,2304]{1,0:T(8,128)(2,1)S(1)}, f32[256,1024]{1,0:T(8,128)S(1)}) custom-call(bf16[1024,1024]{1,0:T(8,128)(2,1)S(1)} %fusion.14.refs_0_, bf16[1024,256]{1,0:T(8,128)(2,1)S(1)} %pad_maximum_fusion.8.refs_1_, bf16[2304,1024]{1,0:T(8,128)(2,1)S(1)} %bitcast.112), custom_call_target="tpu_custom_call" | custom-call | flops 4831838208 | bytes 130000000 | tf_op jit(solution)/shard_map/product_scatter_7/pallas_call | solution.py:561
  614.3 5.4 convolution_convert_fusion
  622.6 10.9 reshape_reshape.13
  633.5 6.1 fusion.1
  649.7 153.6 %reduce-scatter.9.cloned.1.call-done = bf16[24640,128]{1,0:T(8,128)(2,1)} async-done(((bf16[98560,128]{1,0:T(8,128)(2,1)}), bf16[24640,128]{1,0:T(8,128)(2,1)}) %reduce-scatter.9.cloned.1.call-update) | async-done | bytes 6307856 | tf_op jit(solution)/shard_map/reduce_scatter | solution.py:1135
  837.0 9.0 reshape.309.w_ref
  847.2 88.1 %reduce-scatter.7.cloned.1.call-done = bf16[6176,128]{1,0:T(8,128)(2,1)} async-done(((bf16[24704,128]{1,0:T(8,128)(2,1)}), bf16[6176,128]{1,0:T(8,128)(2,1)}) %reduce-scatter.7.cloned.1.call-update) | async-done | bytes 1581072 | tf_op jit(solution)/shard_map/reduce_scatter | solution.py:1135
  945.4 5.5 share_step.5
  961.7 6.2 copy.184
  968.0 7.4 reshape.319.refs_6_.w_ref
  983.8 11.0 reshape.317.refs_4_.w_ref
  1003.2 79.2 %all_gather.15 = f32[1280,128]{1,0:T(8,128)} all-gather(f32[40,128]{1,0:T(8,128)S(1)} %pad_bitcast_fusion), channel_id=1, replica_groups=mesh['dp'=4,'row'=2,'col'=4] {'dp','row','col'}, dimensions={0}, use_global_device_ids=true | all-gather | bytes 675840 | tf_op jit(solution)/shard_map/all_gather | solution.py:1072
  1100.8 8.3 settle.6
  1109.1 7.3 reshape.327
  1119.4 8.5 settle.7
  1136.6 15.2 %settle.4 = bf16[16480,128]{1,0:T(8,128)(2,1)} custom-call(s32[1]{0:T(128)} %bitcast.35.held_ref, bf16[16480,128]{1,0:T(8,128)(2,1)} %bitcast.126, f32[32960,128]{1,0:T(8,128)} %bitcast.116, f32[32960,128]{1,0:T(8,128)} %bitcast.122, bf16[16480,128]{1,0:T(8,128)(2,1)} %reshape.317.refs_4_.w_ref), custom_call_target="tpu_custom_call" | custom-call | flops 21094400 | bytes 25313280 | tf_op jit(solution)/shard_map/settle/pallas_call | solution.py:738
  1151.8 9.1 reshape.325
  1161.0 6.4 copy.191
  1179.6 47.9 %owner_outputs.1 = (f32[32960,128]{1,0:T(8,128)}, f32[32960,128]{1,0:T(8,128)}, f32[32960,128]{1,0:T(8,128)}, f32[32960,128]{1,0:T(8,128)}) custom-call(s32[20]{0:T(128)} %compare_select_fusion.4.which_ref, s32[20]{0:T(128)} %and_select_fusion.block_ref, f32[32960,128]{1,0:T(8,128)} %bitcast.118, f32[32960,128]{1,0:T(8,128)} %bitcast.124, ...), custom_call_target="tpu_custom_call" | custom-call | flops 50626560 | bytes 109690880 | tf_op jit(solution)/shard_map/owner_outputs/pallas_call | solution.py:796
  (363 shorter events, 265.2 us)
Async XLA Ops:
  7.2 141.6 %all-gather.4.cloned.1.call-start = ((), (), s32[]{:S(2)}) async-start(), calls=%async_computation.10 | async-start | bytes 2359296 | tf_op jit(solution)/shard_map/all_gather | solution.py:950
  18.7 43.6 %copy-start.2 = (bf16[2304,1024]{1,0:T(8,128)(2,1)}, bf16[2304,1024]{1,0:T(8,128)(2,1)S(1)}, u32[]{:S(2)}) copy-start(bf16[2304,1024]{1,0:T(8,128)(2,1)S(1)} %pad_maximum_fusion.3.w_ref.refs_2_) | copy-start | bytes 14155780
  63.6 7.2 copy-start
  65.2 7.7 copy-start.24
  65.2 7.7 copy-start.30
  80.8 482.7 %reduce-scatter.5.cloned.1.call-start = ((), (), s32[]{:S(2)}) async-start(), calls=%async_computation.6 | async-start | bytes 2359296 | tf_op jit(solution)/shard_map/reduce_scatter | solution.py:1029
  87.1 8.2 copy-start.69
  88.2 8.3 copy-start.4
  88.2 8.3 copy-start.9
  96.5 50.9 %copy-start.28 = (f32[1024,512]{1,0:T(8,128)S(1)}, f32[1024,512]{1,0:T(8,128)}, u32[]{:S(2)}) copy-start(f32[1024,512]{1,0:T(8,128)} %copy-done.27) | copy-start | bytes 6291460
  167.6 16.5 %copy-start.3 = (bf16[1024,1024]{1,0:T(8,128)(2,1)S(1)}, bf16[1024,1024]{1,0:T(8,128)(2,1)}, u32[]{:S(2)}) copy-start(bf16[1024,1024]{1,0:T(8,128)(2,1)} %w_ref.5) | copy-start | bytes 6291460
  185.3 41.7 %copy-start.33 = (bf16[256,1024]{1,0:T(8,128)(2,1)S(1)}, bf16[256,1024]{1,0:T(8,128)(2,1)}, u32[]{:S(2)}) copy-start(bf16[256,1024]{1,0:T(8,128)(2,1)} %param.13) | copy-start | bytes 1572868
  228.4 46.4 %copy-start.25 = (f32[256,1024]{1,0:T(8,128)}, f32[256,1024]{1,0:T(8,128)S(1)}, u32[]{:S(2)}) copy-start(f32[256,1024]{1,0:T(8,128)S(1)} %get-tuple-element.164) | copy-start | bytes 3145732
  233.2 41.6 %copy-start.8 = (f32[1024,512]{1,0:T(8,128)S(1)}, f32[1024,512]{1,0:T(8,128)}, u32[]{:S(2)}) copy-start(f32[1024,512]{1,0:T(8,128)} %copy-done.7) | copy-start | bytes 6291460
  277.5 45.0 %copy-start.26 = (f32[256,1024]{1,0:T(8,128)S(1)}, f32[256,1024]{1,0:T(8,128)}, u32[]{:S(2)}) copy-start(f32[256,1024]{1,0:T(8,128)} %copy-done.25) | copy-start | bytes 3145732
  325.3 42.5 %copy-start.61 = (f32[256]{0:T(256)}, f32[256]{0:T(256)S(1)}, u32[]{:S(2)}) copy-start(f32[256]{0:T(256)S(1)} %broadcast_multiply_fusion.3) | copy-start | bytes 3076
  413.3 232.3 %reduce-scatter.11.cloned.1.call-start = ((), (), s32[]{:S(2)}) async-start(), calls=%async_computation.9 | async-start | bytes 7864320 | tf_op jit(solution)/shard_map/reduce_scatter | solution.py:1135
  423.3 7.5 copy-start.5
  432.1 64.0 %copy-start.19 = (bf16[1024,1024]{1,0:T(8,128)(2,1)S(1)}, bf16[1024,1024]{1,0:T(8,128)(2,1)}, u32[]{:S(2)}) copy-start(bf16[1024,1024]{1,0:T(8,128)(2,1)} %copy-done.18) | copy-start | bytes 6291460
  508.0 295.3 %reduce-scatter.9.cloned.1.call-start = ((), (), s32[]{:S(2)}) async-start(), calls=%async_computation.8 | async-start | bytes 31539200 | tf_op jit(solution)/shard_map/reduce_scatter | solution.py:1135
  545.0 390.4 %reduce-scatter.7.cloned.1.call-start = ((), (), s32[]{:S(2)}) async-start(), calls=%async_computation.7 | async-start | bytes 7905280 | tf_op jit(solution)/shard_map/reduce_scatter | solution.py:1135
  570.7 43.6 %copy-start.23 = (bf16[1024,1024]{1,0:T(8,128)(2,1)S(1)}, bf16[1024,1024]{1,0:T(8,128)(2,1)}, u32[]{:S(2)}) copy-start(bf16[1024,1024]{1,0:T(8,128)(2,1)} %copy-done.22) | copy-start | bytes 6291460
  822.4 134.1 %all-to-all-start.1 = ((bf16[4,6144,128]{2,1,0:T(8,128)(2,1)}), bf16[4,6144,128]{2,1,0:T(8,128)(2,1)}, u32[]{:S(2)}, u32[]{:S(2)}) async-start(bf16[4,6144,128]{2,1,0:T(8,128)(2,1)} %pad_maximum_fusion.2), calls=%async_computation.5 | async-start | bytes 12582912 | tf_op jit(solution)/shard_map/all_to_all | solution.py:1187
  956.5 175.6 %all-to-all-start = ((bf16[4,6168,128]{2,1,0:T(8,128)(2,1)}), bf16[4,6168,128]{2,1,0:T(8,128)(2,1)}, u32[]{:S(2)}, u32[]{:S(2)}) async-start(bf16[4,6168,128]{2,1,0:T(8,128)(2,1)} %pad_maximum_fusion), calls=%async_computation.3 | async-start | bytes 12632064 | tf_op jit(solution)/shard_map/all_to_all | solution.py:1187
  983.7 12.2 copy-start.71
  983.7 13.1 %copy-start.70 = (f32[6]{0:T(128)S(1)}, f32[6]{0:T(128)}, u32[]{:S(2)}) copy-start(f32[6]{0:T(128)} %copy-done.69) | copy-start | bytes 76
  983.7 13.8 %copy-start.31 = (f32[1024,128]{1,0:T(8,128)S(1)}, f32[1024,128]{1,0:T(8,128)}, u32[]{:S(2)}) copy-start(f32[1024,128]{1,0:T(8,128)} %copy-done.30) | copy-start | bytes 1572868
  983.7 13.8 %copy-start.63 = (pred[1024]{0:T(1024)(128)(4,1)S(1)}, pred[1024]{0:T(1024)(128)(4,1)}, u32[]{:S(2)}) copy-start(pred[1024]{0:T(1024)(128)(4,1)} %copy-done.62) | copy-start | bytes 3076
  983.7 13.8 %copy-start.65 = (pred[1024]{0:T(1024)(128)(4,1)S(1)}, pred[1024]{0:T(1024)(128)(4,1)}, u32[]{:S(2)}) copy-start(pred[1024]{0:T(1024)(128)(4,1)} %copy-done.64) | copy-start | bytes 3076
  983.8 13.7 %copy-start.67 = (pred[1024]{0:T(1024)(128)(4,1)S(1)}, pred[1024]{0:T(1024)(128)(4,1)}, u32[]{:S(2)}) copy-start(pred[1024]{0:T(1024)(128)(4,1)} %copy-done.66) | copy-start | bytes 3076
  1082.4 10.0 copy-start.10
  1089.8 5.7 copy-start.52
  (49 other events, 135.3 us)
Sparse Core Ops, SparseCore 0:
  80.9 34.3 all-gather.3
  413.4 67.6 reduce-scatter.4
  508.1 68.2 reduce-scatter.10
  579.4 223.8 reduce-scatter.8
  806.7 128.5 reduce-scatter.6
